TPU v7x, 32 devices: a whole 2x2x4 slice. The times are simulated.
32 devices in a mesh: leaf: 8 (over z, x), rows: 4 (over y, core).
Axes of the slice: x: 2, y: 2, z: 4, core: 2. Of those that a mesh axis runs over, the one named last changes fastest.
Arguments:
- right_side: float32 [8, 32768], P(None, ('leaf', 'rows')), may hold values from -6 to 6
- diagonal: float32 [32768], P(('leaf', 'rows')), may hold values from 0.5 to 4
- tree_order: int32 [32768], P(('leaf', 'rows')), may hold values from 0 to 32767, as said below
- mid_perm: int32 [8], replicated, may hold values from 0 to 7, each once
- col_factor: bfloat16 [32768, 384], P(('leaf', 'rows')), may hold values from -0.1875 to 0.1875
- mid_factor: bfloat16 [3072, 768], P('leaf', 'rows'), may hold values from -0.15625 to 0.15625
- pre_factor: bfloat16 [3072, 768], P('leaf', 'rows'), may hold values from -0.15625 to 0.15625
- row_factor: bfloat16 [48, 32768], P(None, ('leaf', 'rows')), may hold values from -0.875 to 0.875
Outputs:
- solution: float32 [8, 32768], P(None, ('leaf', 'rows'))
- residual: float32 [8, 32768], P(None, ('leaf', 'rows'))
Inputs may be any that keep to these rules, and one draw needn't show every extreme that they name: `tree_order`: each aligned run of 1024 entries, the run starting at b * 1024, is a permutation of b * 1024 to (b + 1) * 1024 - 1. `mid_perm`: a permutation of 0 to 7.
All inputs are finite; a program needn't handle non-finite values.
Results may differ from a plain program's by a relative error of at most 0.025.
Values may be sent and summed in bfloat16 or wider, within the bound.
No kernel may reach another device: no remote copies, remote signals or barrier semaphores. Data moves between devices by JAX's collectives and lax.ppermute only.
A program may use at most 64 MiB of HBM per device.

v0:
```python
import jax
import jax.numpy as jnp
from jax import lax
from jax.sharding import PartitionSpec as P

ITERS = 2


def curvature(first, second):
    return lax.psum(jnp.sum(first * second, axis=1), ("leaf", "rows"))


def precond_norm(first, second):
    return lax.psum(jnp.sum(first * second, axis=1), ("leaf", "rows"))


def per_device(
    right_side, diagonal, tree_order, mid_perm, col_factor, mid_factor, pre_factor, row_factor
):
    sides, points = right_side.shape
    rank_size = row_factor.shape[0]
    leaves = mid_perm.shape[0]
    row_count = mid_factor.shape[1] // rank_size
    local_index = tree_order % points
    slot_ids = jnp.arange(leaves, dtype=jnp.int32)
    onehot = (mid_perm[:, None] == slot_ids[None, :]).astype(jnp.bfloat16)
    col_split = col_factor.reshape(points, leaves, rank_size)
    own_gram = jnp.dot(row_factor, row_factor.T, preferred_element_type=jnp.float32)
    gram_blocks = lax.all_gather(own_gram[None], "rows", axis=0, tiled=True)

    def gram_apply(field, mid_weight):
        taken_tree = jnp.take(field, local_index, axis=1).astype(jnp.bfloat16)
        coeffs = jnp.einsum(
            "sn,ngk->gsk", taken_tree, col_split, preferred_element_type=jnp.float32
        ).astype(jnp.bfloat16)
        outgoing = jnp.einsum(
            "qg,gsk->qsk", onehot, coeffs, preferred_element_type=jnp.float32
        ).astype(jnp.bfloat16)
        incoming = lax.all_to_all(
            outgoing.reshape(leaves, sides * rank_size),
            "leaf",
            split_axis=0,
            concat_axis=0,
            tiled=True,
        )
        incoming = incoming.reshape(leaves, sides, rank_size)
        weight_split = mid_weight.reshape(leaves, rank_size, row_count * rank_size)
        partial_value = jnp.einsum(
            "lsk,lkm->sm", incoming, weight_split, preferred_element_type=jnp.float32
        )
        totals = lax.psum(partial_value, "rows")
        head_coef = lax.optimization_barrier(totals.astype(jnp.bfloat16)).astype(jnp.float32)
        head_coef = head_coef.reshape(sides, row_count, rank_size)
        gathered = jnp.einsum(
            "sjk,jkm->sjm", head_coef, gram_blocks, precision=lax.Precision.HIGHEST
        )
        gathered = gathered.reshape(sides, row_count * rank_size).astype(jnp.bfloat16)
        returned = jnp.einsum(
            "sm,lkm->lsk", gathered, weight_split, preferred_element_type=jnp.float32
        ).astype(jnp.bfloat16)
        arrived = lax.all_to_all(
            returned.reshape(leaves, sides * rank_size),
            "leaf",
            split_axis=0,
            concat_axis=0,
            tiled=True,
        )
        arrived = arrived.reshape(leaves, sides, rank_size)
        unsent = jnp.einsum(
            "qg,qsk->gsk", onehot, arrived, preferred_element_type=jnp.float32
        ).astype(jnp.bfloat16)
        tree_out = jnp.einsum("gsk,ngk->sn", unsent, col_split, preferred_element_type=jnp.float32)
        return jnp.zeros_like(tree_out).at[:, local_index].set(tree_out)

    def apply_precond(field):
        return field / diagonal[None, :] + gram_apply(field, pre_factor)

    solution = jnp.zeros_like(right_side)
    residual = right_side
    precond = apply_precond(residual)
    direction = precond
    precond_dot = precond_norm(residual, precond)
    for iteration in range(ITERS):
        image = diagonal[None, :] * direction + gram_apply(direction, mid_factor)
        alpha_step = precond_dot / curvature(direction, image)
        solution = solution + alpha_step[:, None] * direction
        residual = residual - alpha_step[:, None] * image
        if iteration + 1 < ITERS:
            precond = apply_precond(residual)
            dot_next = precond_norm(residual, precond)
            direction = precond + (dot_next / precond_dot)[:, None] * direction
            precond_dot = dot_next
    return (solution, residual)


def solution(mesh):
    return jax.shard_map(
        per_device,
        mesh=mesh,
        in_specs=(
            P(None, ("leaf", "rows")),
            P(("leaf", "rows")),
            P(("leaf", "rows")),
            P(),
            P(("leaf", "rows"), None),
            P("leaf", "rows"),
            P("leaf", "rows"),
            P(None, ("leaf", "rows")),
        ),
        out_specs=(P(None, ("leaf", "rows")), P(None, ("leaf", "rows"))),
        check_vma=False,
    )
```

profile of v0, /device:TPU:0, one launch (start us, length us, event | category | flops | bytes accessed | tf_op | source)
XLA Modules:
  0.0 275.6 jit_solution(600486382952462527)
XLA Ops:
  0.6 0.7 compare_and_fusion
  1.4 0.9 copy.167
  2.3 3.2 %gather_fusion = bf16[1024,8]{1,0:T(8,128)(2,1)S(1)} fusion(bf16[8,1024]{0,1:T(8,128)(2,1)S(1)} %copy.167, s32[1024]{0:T(1024)S(1)} %broadcast_clamp_fusion), kind=kCustom, calls=%fused_computation.clone | custom fusion | bytes 36864 | tf_op jit(solution)/shard_map/jit(_take)/gather | solution.py:32
  5.6 1.4 copy.169
  7.1 0.5 fusion
  7.7 0.2 convolution_convert_fusion.7
  8.0 0.5 broadcast.102
  8.5 0.7 reduce.8
  9.2 0.7 reshape.246
  9.9 7.3 %all-to-all-start = ((bf16[8,2,192]{2,1,0:T(2,128)(2,1)}), bf16[8,2,192]{2,1,0:T(2,128)(2,1)S(1)}, u32[]{:S(2)}, u32[]{:S(2)}) async-start(bf16[8,2,192]{2,1,0:T(2,128)(2,1)} %reshape.246), calls=%async_computation | async-start | bytes 16384 | tf_op jit(solution)/shard_map/all_to_all | solution.py:39
  17.5 5.3 %all-gather = f32[192,48]{1,0:T(8,128)S(1)} all-gather(f32[48,48]{1,0:T(8,128)S(1)} %fusion.74), channel_id=2, replica_groups=mesh['leaf'=8,'rows'=4] {'rows'}, dimensions={0}, use_global_device_ids=true | all-gather | bytes 46080 | tf_op jit(solution)/shard_map/all_gather | solution.py:29
  22.8 0.9 all-to-all-done
  23.9 0.2 convolution_bitcast_fusion.7
  24.1 6.3 %psum.56 = bf16[8,192]{1,0:T(8,128)(2,1)S(1)} all-reduce(f32[8,192]{1,0:T(8,128)S(1)} %convolution_bitcast_fusion.7), channel_id=1, replica_groups=mesh['leaf'=8,'rows'=4] {'rows'}, use_global_device_ids=true, to_apply=%region_0.2 | all-reduce | flops 1536 | bytes 9216 | tf_op jit(solution)/shard_map/psum | solution.py:51
  30.8 0.2 fusion.1
  31.1 0.7 reduce.9
  31.9 12.3 %all_to_all.80 = bf16[8,2,192]{2,1,0:T(2,128)(2,1)S(1)} all-to-all(bf16[8,2,192]{2,1,0:T(2,128)(2,1)S(1)} %reshape.248), channel_id=1, replica_groups=mesh['leaf'=8,'rows'=4] {'leaf'}, dimensions={0} | all-to-all | bytes 12288 | tf_op jit(solution)/shard_map/all_to_all | solution.py:61
  44.5 0.3 convolution_bitcast_fusion.3
  44.8 0.2 copy.180
  45.0 3.2 %scatter_custom_fusion = f32[8,1024]{0,1:T(8,128)S(1)} fusion(s32[1024]{0:T(1024)S(1)} %get-tuple-element.16, f32[1024,8]{1,0:T(8,128)S(1)} %copy.180, f32[]{:T(128)} %constant.15.clone.1), kind=kCustom, calls=%fused_computation.54 | custom fusion | bytes 32772 | tf_op jit(solution)/shard_map/scatter | solution.py:73
  48.4 0.6 copy-done.1
  49.2 3.2 %gather_fusion.1 = bf16[1024,8]{1,0:T(8,128)(2,1)S(1)} fusion(bf16[8,1024]{0,1:T(8,128)(2,1)S(1)} %copy.182, s32[1024]{0:T(1024)S(1)} %broadcast_clamp_fusion), kind=kCustom, calls=%fused_computation.1.clone | custom fusion | bytes 36864 | tf_op jit(solution)/shard_map/jit(_take)/gather | solution.py:32
  52.5 0.5 fusion.2
  53.0 0.2 convolution_convert_fusion.5
  53.3 0.7 reduce.10
  54.0 0.7 reshape.250
  54.7 3.3 %all-to-all-start.2 = ((bf16[8,2,192]{2,1,0:T(2,128)(2,1)}), bf16[8,2,192]{2,1,0:T(2,128)(2,1)S(1)}, u32[]{:S(2)}, u32[]{:S(2)}) async-start(bf16[8,2,192]{2,1,0:T(2,128)(2,1)} %reshape.250), calls=%async_computation.2 | async-start | bytes 16384 | tf_op jit(solution)/shard_map/all_to_all | solution.py:39
  58.2 6.3 %all-to-all-done.2 = bf16[8,2,192]{2,1,0:T(2,128)(2,1)S(1)} async-done(((bf16[8,2,192]{2,1,0:T(2,128)(2,1)}), bf16[8,2,192]{2,1,0:T(2,128)(2,1)S(1)}, u32[]{:S(2)}, u32[]{:S(2)}) %all-to-all-start.2) | async-done | bytes 6176 | tf_op jit(solution)/shard_map/all_to_all | solution.py:39
  64.7 0.2 convolution_bitcast_fusion.6
  64.9 6.0 %psum.58 = bf16[8,192]{1,0:T(8,128)(2,1)S(1)} all-reduce(f32[8,192]{1,0:T(8,128)S(1)} %convolution_bitcast_fusion.6), channel_id=1, replica_groups=mesh['leaf'=8,'rows'=4] {'rows'}, use_global_device_ids=true, to_apply=%region_4.6 | all-reduce | flops 1536 | bytes 9216 | tf_op jit(solution)/shard_map/psum | solution.py:51
  71.6 0.7 reduce.11
  72.3 8.9 %all_to_all.81 = bf16[8,2,192]{2,1,0:T(2,128)(2,1)S(1)} all-to-all(bf16[8,2,192]{2,1,0:T(2,128)(2,1)S(1)} %reshape.252), channel_id=1, replica_groups=mesh['leaf'=8,'rows'=4] {'leaf'}, dimensions={0} | all-to-all | bytes 12288 | tf_op jit(solution)/shard_map/all_to_all | solution.py:61
  81.6 0.3 convolution_bitcast_fusion.2
  81.8 0.2 copy.194
  82.0 3.2 %scatter_custom_fusion.1 = f32[8,1024]{0,1:T(8,128)S(1)} fusion(s32[1024]{0:T(1024)S(1)} %get-tuple-element.16, f32[1024,8]{1,0:T(8,128)S(1)} %copy.194, f32[]{:T(128)} %constant.15.clone.1), kind=kCustom, calls=%fused_computation.52 | custom fusion | bytes 32772 | tf_op jit(solution)/shard_map/scatter | solution.py:73
  85.6 38.2 %all-reduce = (f32[8]{0:T(128)S(1)}, f32[8]{0:T(128)S(1)}) all-reduce(f32[8]{0:T(128)S(1)} %get-tuple-element.12, f32[8]{0:T(128)S(1)} %get-tuple-element.11), channel_id=1, replica_groups=mesh['leaf'=8,'rows'=4] {'leaf','rows'}, use_global_device_ids=true, to_apply=%region_3.5 | all-reduce | flops 16 | bytes 128 | tf_op jit(solution)/shard_map/psum | solution.py:14
  124.0 3.2 %gather_fusion.2 = bf16[1024,8]{1,0:T(8,128)(2,1)S(1)} fusion(bf16[8,1024]{0,1:T(8,128)(2,1)S(1)} %copy.196, s32[1024]{0:T(1024)S(1)} %broadcast_clamp_fusion), kind=kCustom, calls=%fused_computation.2.clone | custom fusion | bytes 36864 | tf_op jit(solution)/shard_map/jit(_take)/gather | solution.py:32
  127.4 0.5 fusion.4
  127.9 0.2 convolution_convert_fusion.3
  128.2 0.7 reduce.12
  129.0 11.0 %all_to_all.82 = bf16[8,2,192]{2,1,0:T(2,128)(2,1)S(1)} all-to-all(bf16[8,2,192]{2,1,0:T(2,128)(2,1)S(1)} %reshape.254), channel_id=1, replica_groups=mesh['leaf'=8,'rows'=4] {'leaf'}, dimensions={0} | all-to-all | bytes 12288 | tf_op jit(solution)/shard_map/all_to_all | solution.py:39
  140.1 0.2 convolution_bitcast_fusion.5
  140.3 6.1 %psum.60 = bf16[8,192]{1,0:T(8,128)(2,1)S(1)} all-reduce(f32[8,192]{1,0:T(8,128)S(1)} %convolution_bitcast_fusion.5), channel_id=1, replica_groups=mesh['leaf'=8,'rows'=4] {'rows'}, use_global_device_ids=true, to_apply=%region_8.10 | all-reduce | flops 1536 | bytes 9216 | tf_op jit(solution)/shard_map/psum | solution.py:51
  147.1 0.7 reduce.13
  147.8 8.9 %all_to_all.83 = bf16[8,2,192]{2,1,0:T(2,128)(2,1)S(1)} all-to-all(bf16[8,2,192]{2,1,0:T(2,128)(2,1)S(1)} %reshape.256), channel_id=1, replica_groups=mesh['leaf'=8,'rows'=4] {'leaf'}, dimensions={0} | all-to-all | bytes 12288 | tf_op jit(solution)/shard_map/all_to_all | solution.py:61
  157.1 0.3 convolution_bitcast_fusion.1
  157.3 0.2 copy.207
  157.5 3.4 %scatter_custom_fusion.2 = f32[8,1024]{0,1:T(8,128)S(1)} fusion(s32[1024]{0:T(1024)S(1)} %get-tuple-element.16, f32[1024,8]{1,0:T(8,128)S(1)} %copy.207, f32[]{:T(128)} %constant.15.clone.1), kind=kCustom, calls=%fused_computation.50 | custom fusion | bytes 32772 | tf_op jit(solution)/shard_map/scatter | solution.py:73
  161.2 38.2 %psum.61 = f32[8]{0:T(128)S(1)} all-reduce(f32[8]{0:T(128)S(1)} %multiply_reduce_fusion.1), channel_id=1, replica_groups=mesh['leaf'=8,'rows'=4] {'leaf','rows'}, use_global_device_ids=true, to_apply=%region_11.13 | all-reduce | flops 8 | bytes 64 | tf_op jit(solution)/shard_map/psum | solution.py:14
  199.7 3.2 %gather_fusion.3 = bf16[1024,8]{1,0:T(8,128)(2,1)S(1)} fusion(bf16[8,1024]{0,1:T(8,128)(2,1)S(1)} %copy.209, s32[1024]{0:T(1024)S(1)} %broadcast_clamp_fusion), kind=kCustom, calls=%fused_computation.3.clone | custom fusion | bytes 36864 | tf_op jit(solution)/shard_map/jit(_take)/gather | solution.py:32
  203.0 0.5 fusion.6
  203.5 0.2 convolution_convert_fusion.1
  203.8 0.7 reduce.14
  204.6 11.0 %all_to_all.84 = bf16[8,2,192]{2,1,0:T(2,128)(2,1)S(1)} all-to-all(bf16[8,2,192]{2,1,0:T(2,128)(2,1)S(1)} %reshape.258), channel_id=1, replica_groups=mesh['leaf'=8,'rows'=4] {'leaf'}, dimensions={0} | all-to-all | bytes 12288 | tf_op jit(solution)/shard_map/all_to_all | solution.py:39
  215.8 0.2 convolution_bitcast_fusion.4
  216.0 6.1 %psum.62 = bf16[8,192]{1,0:T(8,128)(2,1)S(1)} all-reduce(f32[8,192]{1,0:T(8,128)S(1)} %convolution_bitcast_fusion.4), channel_id=1, replica_groups=mesh['leaf'=8,'rows'=4] {'rows'}, use_global_device_ids=true, to_apply=%region_12.14 | all-reduce | flops 1536 | bytes 9216 | tf_op jit(solution)/shard_map/psum | solution.py:51
  222.4 0.2 fusion.7
  222.7 0.7 reduce.15
  223.5 8.9 %all_to_all.85 = bf16[8,2,192]{2,1,0:T(2,128)(2,1)S(1)} all-to-all(bf16[8,2,192]{2,1,0:T(2,128)(2,1)S(1)} %reshape.260), channel_id=1, replica_groups=mesh['leaf'=8,'rows'=4] {'leaf'}, dimensions={0} | all-to-all | bytes 12288 | tf_op jit(solution)/shard_map/all_to_all | solution.py:61
  232.7 0.3 convolution_bitcast_fusion
  233.0 0.2 copy.220
  233.2 3.2 %scatter_custom_fusion.3 = f32[8,1024]{0,1:T(8,128)S(1)} fusion(s32[1024]{0:T(1024)S(1)} %get-tuple-element.16, f32[1024,8]{1,0:T(8,128)S(1)} %copy.220, f32[]{:T(128)} %constant.15.clone.1), kind=kCustom, calls=%fused_computation.48 | custom fusion | bytes 32772 | tf_op jit(solution)/shard_map/scatter | solution.py:73
  236.7 38.2 %psum.63 = f32[8]{0:T(128)S(1)} all-reduce(f32[8]{0:T(128)S(1)} %multiply_reduce_fusion), channel_id=1, replica_groups=mesh['leaf'=8,'rows'=4] {'leaf','rows'}, use_global_device_ids=true, to_apply=%region_15.17 | all-reduce | flops 8 | bytes 64 | tf_op jit(solution)/shard_map/psum | solution.py:10
  274.9 0.7 multiply_subtract_fusion
  (99 shorter events, 8.3 us)
Async XLA Ops:
  0.6 16.6 %copy-start = (bf16[48,1024]{1,0:T(8,128)(2,1)S(1)}, bf16[48,1024]{1,0:T(8,128)(2,1)}, u32[]{:S(2)}) copy-start(bf16[48,1024]{1,0:T(8,128)(2,1)} %param.17) | copy-start | bytes 294916
  7.1 0.7 copy-start.5
  7.9 9.4 %copy-start.3 = (bf16[384,192]{0,1:T(8,128)(2,1)S(1)}, bf16[384,192]{0,1:T(8,128)(2,1)}, u32[]{:S(2)}) copy-start(bf16[384,192]{0,1:T(8,128)(2,1)} %param.16) | copy-start | bytes 442372
  9.9 13.8 %all-to-all-start = ((bf16[8,2,192]{2,1,0:T(2,128)(2,1)}), bf16[8,2,192]{2,1,0:T(2,128)(2,1)S(1)}, u32[]{:S(2)}, u32[]{:S(2)}) async-start(bf16[8,2,192]{2,1,0:T(2,128)(2,1)} %reshape.246), calls=%async_computation | async-start | bytes 16384 | tf_op jit(solution)/shard_map/all_to_all | solution.py:39
  48.3 0.8 copy-start.1
  48.3 0.8 copy-start.2
  52.5 5.5 %copy-start.4 = (bf16[384,192]{0,1:T(8,128)(2,1)S(1)}, bf16[384,192]{0,1:T(8,128)(2,1)}, u32[]{:S(2)}) copy-start(bf16[384,192]{0,1:T(8,128)(2,1)} %param.15) | copy-start | bytes 442372
  54.7 9.8 %all-to-all-start.2 = ((bf16[8,2,192]{2,1,0:T(2,128)(2,1)}), bf16[8,2,192]{2,1,0:T(2,128)(2,1)S(1)}, u32[]{:S(2)}, u32[]{:S(2)}) async-start(bf16[8,2,192]{2,1,0:T(2,128)(2,1)} %reshape.250), calls=%async_computation.2 | async-start | bytes 16384 | tf_op jit(solution)/shard_map/all_to_all | solution.py:39
where the time goes:
time: 277 us; the launch traced here: 276 us
  blocking collectives  205 us (74%)
  local copies, waits for them, and re-layouts  37.2 us (13%)
  starting transfers between devices  10.6 us (4%)
  other arithmetic  7.88 us (3%)
  waiting for transfers between devices  7.17 us (3%)
  matrix products  6.49 us (2%)
    psum x2, blocking collectives, precond_norm(): return lax.psum(jnp.sum(first * second, axis=1), ('leaf', 'rows'))  76.4 us
    all_to_all x4, blocking collectives, gram_apply(): lax.all_to_all(returned.reshape(leaves, sides * rank_size), 'leaf', split...  38.9 us
    psum x1, blocking collectives, curvature(): return lax.psum(jnp.sum(first * second, axis=1), ('leaf', 'rows'))  38.2 us
    psum x4, blocking collectives, gram_apply(): totals = lax.psum(partial_value, 'rows')  24.5 us
    all_to_all x2, blocking collectives, gram_apply(): lax.all_to_all(outgoing.reshape(leaves, sides * rank_size), 'leaf', split...  21.9 us
    scatter x8, local copies, waits for them, and re-layouts, gram_apply(): return jnp.zeros_like(tree_out).at[:, local_index].set(tree_out)  13.7 us
    gather x8, local copies, waits for them, and re-layouts, gram_apply(): taken_tree = jnp.take(field, local_index, axis=1).astype(jnp.bfloat16)  13.3 us
    all_to_all x2, starting transfers between devices, gram_apply(): lax.all_to_all(outgoing.reshape(leaves, sides * rank_size), 'leaf', split...  10.6 us
  transfers between devices with their start and end apart: 2, of which 2 were waited for; matrix products, arithmetic and copies ran while one was open for 0% of the time, Pallas kernels for 0%

commit v1 on v0

v1 whole, which is shorter than its diff:
```python
import jax
import jax.numpy as jnp
from jax import lax
from jax.sharding import PartitionSpec as P

ITERS = 2
LANES = 128


def widen(values, width):
    pads = [(0, 0)] * (values.ndim - 1) + [(0, width - values.shape[-1])]
    return jnp.pad(values, pads)


def per_device(
    right_side, diagonal, tree_order, mid_perm, col_factor, mid_factor, pre_factor, row_factor
):
    sides, points = right_side.shape
    rank_size = row_factor.shape[0]
    leaves = mid_perm.shape[0]
    row_count = mid_factor.shape[1] // rank_size
    width = -(-(rank_size + 1) // LANES) * LANES
    row = lax.axis_index("rows")
    shifts = jnp.arange(row_count, dtype=jnp.int32)
    sources = (row - shifts) % row_count

    def gather_rows(block):
        pieces = [block]
        for shift in range(1, row_count):
            ring = [(i, (i + shift) % row_count) for i in range(row_count)]
            pieces.append(lax.ppermute(block, "rows", ring))
        return [piece.reshape(leaves, rank_size, row_count * rank_size) for piece in pieces]

    own_gram = jnp.dot(row_factor, row_factor.T, preferred_element_type=jnp.float32)
    gram_blocks = lax.all_gather(own_gram[None], "rows", axis=0, tiled=True)
    pre_pieces = gather_rows(pre_factor)
    mid_pieces = gather_rows(mid_factor)

    local_index = tree_order % points
    point_ids = jnp.arange(points, dtype=jnp.int32)
    place = (point_ids[:, None] == local_index[None, :]).astype(jnp.bfloat16)
    slot_ids = jnp.arange(leaves, dtype=jnp.int32)
    onehot = (mid_perm[:, None] == slot_ids[None, :]).astype(jnp.bfloat16)
    columns = jnp.dot(place, col_factor, preferred_element_type=jnp.float32).astype(jnp.bfloat16)
    columns = columns.reshape(points, leaves, rank_size)
    columns = jnp.einsum(
        "qg,ngk->nqk", onehot, columns, preferred_element_type=jnp.float32
    ).astype(jnp.bfloat16)

    def gram_apply(field, pieces, local_dot):
        coeffs = jnp.einsum(
            "sn,nqk->qsk", field.astype(jnp.bfloat16), columns, preferred_element_type=jnp.float32
        )
        dots = jnp.broadcast_to(local_dot[None, :, None], (leaves, sides, 1))
        outgoing = widen(jnp.concatenate([coeffs, dots], axis=2), width)
        outgoing = jnp.broadcast_to(
            outgoing[:, None], (leaves, row_count, sides, width)
        ).reshape(leaves * row_count, sides, width)
        incoming = lax.all_to_all(
            outgoing, ("leaf", "rows"), split_axis=0, concat_axis=0, tiled=True
        )
        local_total = jnp.sum(incoming[:, :, rank_size], axis=0)
        incoming = incoming[:, :, :rank_size].astype(jnp.bfloat16)
        incoming = incoming.reshape(leaves, row_count, sides, rank_size)
        incoming = jnp.take(incoming, sources, axis=1)
        totals = 0.0
        for shift in range(row_count):
            totals = totals + jnp.einsum(
                "lsk,lkm->sm",
                incoming[:, shift],
                pieces[shift],
                preferred_element_type=jnp.float32,
            )
        head_coef = totals.astype(jnp.bfloat16).astype(jnp.float32)
        head_coef = head_coef.reshape(sides, row_count, rank_size)
        gathered = jnp.einsum(
            "sjk,jkm->sjm", head_coef, gram_blocks, precision=lax.Precision.HIGHEST
        )
        own_dot = jnp.sum(head_coef * gathered, axis=(1, 2))
        gathered = gathered.reshape(sides, row_count * rank_size).astype(jnp.bfloat16)
        returned = jnp.einsum(
            "sm,lkm->lsk", gathered, pieces[0], preferred_element_type=jnp.float32
        )
        dots = jnp.broadcast_to(own_dot[None, :, None], (leaves, sides, 1))
        returned = widen(jnp.concatenate([returned, dots], axis=2), width)
        arrived = lax.all_to_all(returned, "leaf", split_axis=0, concat_axis=0, tiled=True)
        total_dot = local_total + jnp.sum(arrived[:, :, rank_size], axis=0)
        unsent = arrived[:, :, :rank_size].astype(jnp.bfloat16)
        image = jnp.einsum("qsk,nqk->sn", unsent, columns, preferred_element_type=jnp.float32)
        return image, total_dot

    def apply_precond(field):
        scaled = field / diagonal[None, :]
        image, total = gram_apply(field, pre_pieces, jnp.sum(field * scaled, axis=1))
        return scaled + image, total

    def apply_system(field):
        scaled = field * diagonal[None, :]
        image, total = gram_apply(field, mid_pieces, jnp.sum(field * scaled, axis=1))
        return scaled + image, total

    solution = jnp.zeros_like(right_side)
    residual = right_side
    direction, residual_dot = apply_precond(residual)
    for iteration in range(ITERS):
        image, curvature = apply_system(direction)
        alpha_step = residual_dot / curvature
        solution = solution + alpha_step[:, None] * direction
        residual = residual - alpha_step[:, None] * image
        if iteration + 1 < ITERS:
            precond, dot_next = apply_precond(residual)
            direction = precond + (dot_next / residual_dot)[:, None] * direction
            residual_dot = dot_next
    return (solution, residual)


def solution(mesh):
    return jax.shard_map(
        per_device,
        mesh=mesh,
        in_specs=(
            P(None, ("leaf", "rows")),
            P(("leaf", "rows")),
            P(("leaf", "rows")),
            P(),
            P(("leaf", "rows"), None),
            P("leaf", "rows"),
            P("leaf", "rows"),
            P(None, ("leaf", "rows")),
        ),
        out_specs=(P(None, ("leaf", "rows")), P(None, ("leaf", "rows"))),
        check_vma=False,
    )
```

time: 277 us -> 115 us (0.42)
  blocking collectives: 205 us -> 25.3 us
  local copies, waits for them, and re-layouts: 37.2 us -> 9.15 us
  waiting for transfers between devices: 7.17 us -> 29.4 us
  starting transfers between devices: 10.6 us -> 27.4 us
  matrix products: 6.49 us -> 11.7 us
    psum x7 -> x0, blocking collectives: 139 us -> none  [the longest x2 76.4 us: precond_norm(): return lax.psum(jnp.sum(first * second, axis=1), ('leaf', 'rows'))]
    all_to_all x6 -> x2, blocking collectives: 60.9 us -> 19.8 us  [gram_apply(): lax.all_to_all(outgoing, ('leaf', 'rows'), split_axis=0, concat_axis=0, t...]
    all_to_all x2 -> x6, waiting for transfers between devices: 7.17 us -> 29.4 us  [the longest x4 24 us: gram_apply(): lax.all_to_all(returned, 'leaf', split_axis=0, concat_axis=0, tiled=True)]
    scatter x8 -> x0, local copies, waits for them, and re-layouts: 13.7 us -> none  [gram_apply(): return jnp.zeros_like(tree_out).at[:, local_index].set(tree_out)]
    all_to_all x2 -> x6, starting transfers between devices: 10.6 us -> 21.9 us  [the longest x4 14 us: gram_apply(): lax.all_to_all(returned, 'leaf', split_axis=0, concat_axis=0, tiled=True)]
    gather x8 -> x4, local copies, waits for them, and re-layouts: 13.3 us -> 2.28 us  [gram_apply(): incoming = jnp.take(incoming, sources, axis=1)]
    all_to_all x16 -> x0, other arithmetic: 5.83 us -> none  [the longest x8 2.92 us: gram_apply(): lax.all_to_all(returned.reshape(leaves, sides * rank_size), 'leaf', split...]
    unnamed x32 -> x26, local copies, waits for them, and re-layouts: 6 us -> 0.47 us
  transfers between devices with their start and end apart: 2 -> 12, of which waited for: 2 -> 6; matrix products, arithmetic and copies ran while one was open for 0% -> 10% of each run, Pallas kernels for 0% -> 0%
where the time goes in v1:
time: 115 us; the launch traced here: 114 us
  waiting for transfers between devices  29.4 us (26%)
  starting transfers between devices  27.4 us (24%)
  blocking collectives  25.3 us (22%)
  matrix products  11.7 us (10%)
  other arithmetic  9.92 us (9%)
  local copies, waits for them, and re-layouts  9.15 us (8%)
    all_to_all x4, waiting for transfers between devices, gram_apply(): lax.all_to_all(returned, 'leaf', split_axis=0, concat_axis=0, tiled=True)  24 us
    all_to_all x2, blocking collectives, gram_apply(): lax.all_to_all(outgoing, ('leaf', 'rows'), split_axis=0, concat_axis=0, t...  19.8 us
    all_to_all x4, starting transfers between devices, gram_apply(): lax.all_to_all(returned, 'leaf', split_axis=0, concat_axis=0, tiled=True)  14 us
    all_to_all x2, starting transfers between devices, gram_apply(): lax.all_to_all(outgoing, ('leaf', 'rows'), split_axis=0, concat_axis=0, t...  7.92 us
    ppermute x6, starting transfers between devices, gather_rows(): pieces.append(lax.ppermute(block, 'rows', ring))  5.48 us
    all_gather x1, blocking collectives, per_device(): gram_blocks = lax.all_gather(own_gram[None], 'rows', axis=0, tiled=True)  5.47 us
    all_to_all x2, waiting for transfers between devices, gram_apply(): lax.all_to_all(outgoing, ('leaf', 'rows'), split_axis=0, concat_axis=0, t...  5.4 us
    dot_general x4, matrix products, gram_apply(): jnp.einsum('qsk,nqk->sn', unsent, columns, preferred_element_type=jnp.flo...  3.64 us
  transfers between devices with their start and end apart: 12, of which 6 were waited for; matrix products, arithmetic and copies ran while one was open for 10% of the time, Pallas kernels for 0%

profile of v1, /device:TPU:0, one launch (start us, length us, event | category | flops | bytes accessed | tf_op | source)
XLA Modules:
  0.0 113.9 jit_solution(2663293570394098638)
XLA Ops:
  0.6 2.5 %collective-permute-start.2 = (bf16[384,192]{0,1:T(8,128)(2,1)}, bf16[384,192]{0,1:T(8,128)(2,1)S(1)}, u32[]{:S(2)}, u32[]{:S(2)}) collective-permute-start(bf16[384,192]{0,1:T(8,128)(2,1)} %param.16), channel_id=1, source_target_pairs={{0,3},{1,0},{2,1},{3,2},{4,7},{5,4},{6,5},{7,6},{8,11},{9,8},{10,9... | collective-permute-start | bytes 442376 | tf_op jit(solution)/shard_map/ppermute | solution.py:31
  3.1 1.1 collective-permute-start.1
  4.2 0.7 add_select_fusion
  4.9 1.1 fusion.2
  6.1 0.6 fusion.3
  6.9 0.3 convolution_bitcast_fusion.3
  7.6 0.7 broadcast_in_dim.36
  8.2 5.3 %all-to-all-start = ((f32[32,8,128]{2,1,0:T(8,128)}), f32[32,8,128]{2,1,0:T(8,128)S(1)}, u32[]{:S(2)}, u32[]{:S(2)}) async-start(f32[32,8,128]{2,1,0:T(8,128)} %bitcast.5), calls=%async_computation | async-start | bytes 262144 | tf_op jit(solution)/shard_map/all_to_all | solution.py:59
  13.9 5.5 %all-gather = f32[192,48]{1,0:T(8,128)S(1)} all-gather(f32[48,48]{1,0:T(8,128)S(1)} %fusion.58), channel_id=2, replica_groups=mesh['leaf'=8,'rows'=4] {'rows'}, dimensions={0}, use_global_device_ids=true | all-gather | bytes 46080 | tf_op jit(solution)/shard_map/all_gather | solution.py:35
  19.9 1.9 %all-to-all-done = f32[32,8,128]{2,1,0:T(8,128)S(1)} async-done(((f32[32,8,128]{2,1,0:T(8,128)}), f32[32,8,128]{2,1,0:T(8,128)S(1)}, u32[]{:S(2)}, u32[]{:S(2)}) %all-to-all-start) | async-done | bytes 131104 | tf_op jit(solution)/shard_map/all_to_all | solution.py:59
  21.8 0.6 gather_fusion
  22.6 0.2 convolution_bitcast_fusion.31
  22.8 0.2 fusion.24
  23.0 0.2 fusion.25
  23.3 0.3 fusion.57
  23.9 0.7 select_maximum_fusion.6
  24.7 3.9 %all-to-all-start.1 = ((f32[8,8,128]{2,1,0:T(8,128)}), f32[8,8,128]{2,1,0:T(8,128)S(1)}, u32[]{:S(2)}, u32[]{:S(2)}) async-start(f32[8,8,128]{2,1,0:T(8,128)} %select_maximum_fusion.6), calls=%async_computation.1 | async-start | bytes 65536 | tf_op jit(solution)/shard_map/all_to_all | solution.py:86
  28.6 1.1 collective-permute-start.5
  29.7 0.8 collective-permute-start.4
  30.5 4.8 %all-to-all-done.1 = f32[8,8,128]{2,1,0:T(8,128)S(1)} async-done(((f32[8,8,128]{2,1,0:T(8,128)}), f32[8,8,128]{2,1,0:T(8,128)S(1)}, u32[]{:S(2)}, u32[]{:S(2)}) %all-to-all-start.1) | async-done | bytes 32800 | tf_op jit(solution)/shard_map/all_to_all | solution.py:86
  35.3 0.7 fusion.34
  35.9 0.3 convolution_bitcast_fusion.2
  36.5 0.7 broadcast_in_dim.40
  37.2 2.6 %all-to-all-start.2 = ((f32[32,8,128]{2,1,0:T(8,128)}), f32[32,8,128]{2,1,0:T(8,128)S(1)}, u32[]{:S(2)}, u32[]{:S(2)}) async-start(f32[32,8,128]{2,1,0:T(8,128)} %bitcast.26), calls=%async_computation.2 | async-start | bytes 262144 | tf_op jit(solution)/shard_map/all_to_all | solution.py:59
  40.1 1.0 copy.146
  41.2 1.0 copy.147
  42.2 0.7 slice_reduce_fusion.3
  42.9 1.5 %slice_reduce_fusion.7 = f32[8]{0:T(128)} fusion(f32[8,8,128]{2,1,0:T(8,128)} %copy-done.8), kind=kLoop, calls=%fused_computation.101 | loop fusion | flops 56 | bytes 288 | tf_op jit(solution)/shard_map/reduce_sum | solution.py:87
  44.5 3.5 %all-to-all-done.2 = f32[32,8,128]{2,1,0:T(8,128)S(1)} async-done(((f32[32,8,128]{2,1,0:T(8,128)}), f32[32,8,128]{2,1,0:T(8,128)S(1)}, u32[]{:S(2)}, u32[]{:S(2)}) %all-to-all-start.2) | async-done | bytes 131104 | tf_op jit(solution)/shard_map/all_to_all | solution.py:59
  48.0 0.6 gather_fusion.1
  48.8 0.2 convolution_bitcast_fusion.27
  49.0 0.2 fusion.21
  49.2 0.2 fusion.26
  49.5 0.3 fusion.56
  50.1 0.7 select_maximum_fusion.4
  50.9 3.3 %all-to-all-start.3 = ((f32[8,8,128]{2,1,0:T(8,128)}), f32[8,8,128]{2,1,0:T(8,128)S(1)}, u32[]{:S(2)}, u32[]{:S(2)}) async-start(f32[8,8,128]{2,1,0:T(8,128)} %select_maximum_fusion.4), calls=%async_computation.3 | async-start | bytes 65536 | tf_op jit(solution)/shard_map/all_to_all | solution.py:86
  54.2 0.2 slice_reduce_fusion.2
  54.4 6.4 %all-to-all-done.3 = f32[8,8,128]{2,1,0:T(8,128)S(1)} async-done(((f32[8,8,128]{2,1,0:T(8,128)}), f32[8,8,128]{2,1,0:T(8,128)S(1)}, u32[]{:S(2)}, u32[]{:S(2)}) %all-to-all-start.3) | async-done | bytes 32800 | tf_op jit(solution)/shard_map/all_to_all | solution.py:86
  61.0 1.3 %add_divide_fusion.1 = (f32[8]{0:T(128)S(1)}, f32[8]{0:T(128)}) fusion(f32[8]{0:T(128)S(1)} %slice_reduce_fusion.2, f32[8]{0:T(128)S(1)} %slice_reduce_fusion.6, f32[8]{0:T(128)} %slice_reduce_fusion.3, f32[8]{0:T(128)} %slice_reduce_fusion.7), kind=kLoop, calls=%fused_computation.155 | loop fusion | flops 24 | bytes 192 | tf_op jit(solution)/shard_map/div | solution.py:107
  62.3 1.2 %multiply_reduce_fusion = (f32[8]{0:T(128)}, f32[8,1024]{1,0:T(8,128)S(1)}) fusion(f32[1024]{0:T(1024)S(1)} %copy-done.9, f32[8,1024]{1,0:T(8,128)S(1)} %copy-done.7, bf16[1024,8,48]{0,1,2:T(8,128)(2,1)S(1)} %fusion.3, f32[8,8,128]{2,1,0:T(8,128)S(1)} %all-to-all-done.3, f32[8,1024]{1,0:T(8,128)S(1)} %get-tuple-element.16, f32[8]{0:T(128)S(1)} %get-tuple-element.5), kind=kOutput, calls=%fused_computation.106 | convolution fusion | flops 6348792 | bytes 905760 | tf_op jit(solution)/shard_map/qsk,nqk->sn/dot_general | solution.py:89
  63.5 0.3 convolution_bitcast_fusion.1
  63.9 0.7 broadcast_in_dim.42
  64.8 9.9 %all_to_all.40 = f32[32,8,128]{2,1,0:T(8,128)S(1)} all-to-all(f32[32,8,128]{2,1,0:T(8,128)S(1)} %bitcast.265), channel_id=1, replica_groups=mesh['leaf'=8,'rows'=4] {'leaf','rows'}, dimensions={0} | all-to-all | bytes 262144 | tf_op jit(solution)/shard_map/all_to_all | solution.py:59
  74.7 0.6 gather_fusion.2
  75.7 0.2 fusion.18
  75.9 0.2 fusion.27
  76.2 0.3 fusion.55
  76.8 0.7 select_maximum_fusion.2
  77.6 3.3 %all-to-all-start.5 = ((f32[8,8,128]{2,1,0:T(8,128)}), f32[8,8,128]{2,1,0:T(8,128)S(1)}, u32[]{:S(2)}, u32[]{:S(2)}) async-start(f32[8,8,128]{2,1,0:T(8,128)} %select_maximum_fusion.2), calls=%async_computation.5 | async-start | bytes 65536 | tf_op jit(solution)/shard_map/all_to_all | solution.py:86
  80.9 0.2 slice_reduce_fusion.1
  81.1 6.4 %all-to-all-done.5 = f32[8,8,128]{2,1,0:T(8,128)S(1)} async-done(((f32[8,8,128]{2,1,0:T(8,128)}), f32[8,8,128]{2,1,0:T(8,128)S(1)}, u32[]{:S(2)}, u32[]{:S(2)}) %all-to-all-start.5) | async-done | bytes 32800 | tf_op jit(solution)/shard_map/all_to_all | solution.py:86
  87.8 0.7 fusion.35
  88.4 0.3 convolution_bitcast_fusion
  89.1 9.9 %all_to_all.41 = f32[32,8,128]{2,1,0:T(8,128)S(1)} all-to-all(f32[32,8,128]{2,1,0:T(8,128)S(1)} %bitcast.266), channel_id=1, replica_groups=mesh['leaf'=8,'rows'=4] {'leaf','rows'}, dimensions={0} | all-to-all | bytes 262144 | tf_op jit(solution)/shard_map/all_to_all | solution.py:59
  99.0 0.6 gather_fusion.3
  100.0 0.2 fusion.15
  100.2 0.2 fusion.28
  100.5 0.3 fusion.54
  101.1 0.7 select_maximum_fusion
  101.8 3.3 %all-to-all-start.7 = ((f32[8,8,128]{2,1,0:T(8,128)}), f32[8,8,128]{2,1,0:T(8,128)S(1)}, u32[]{:S(2)}, u32[]{:S(2)}) async-start(f32[8,8,128]{2,1,0:T(8,128)} %select_maximum_fusion), calls=%async_computation.7 | async-start | bytes 65536 | tf_op jit(solution)/shard_map/all_to_all | solution.py:86
  105.2 0.2 slice_reduce_fusion
  105.4 6.4 %all-to-all-done.7 = f32[8,8,128]{2,1,0:T(8,128)S(1)} async-done(((f32[8,8,128]{2,1,0:T(8,128)}), f32[8,8,128]{2,1,0:T(8,128)S(1)}, u32[]{:S(2)}, u32[]{:S(2)}) %all-to-all-start.7) | async-done | bytes 32800 | tf_op jit(solution)/shard_map/all_to_all | solution.py:86
  112.0 0.7 multiply_add_fusion
  112.7 1.2 %fusion.6 = f32[8,1024]{1,0:T(8,128)} fusion(f32[8,1024]{1,0:T(8,128)S(1)} %copy-done.5, bf16[1024,8,48]{0,1,2:T(8,128)(2,1)S(1)} %fusion.3, f32[8,1024]{1,0:T(8,128)S(1)} %get-tuple-element.20, f32[8,8,128]{2,1,0:T(8,128)S(1)} %all-to-all-done.7, f32[8]{0:T(128)S(1)} %add_divide_fusion, f32[1024]{0:T(1024)S(1)} %copy-done.9), kind=kOutput, calls=%fused_computation.17 | convolution fusion | flops 6324224 | bytes 905728 | tf_op jit(solution)/shard_map/qsk,nqk->sn/dot_general | solution.py:89
  (95 shorter events, 6.1 us)
Async XLA Ops:
  0.6 4.3 %copy-start = (bf16[1024,384]{1,0:T(8,128)(2,1)S(1)}, bf16[1024,384]{1,0:T(8,128)(2,1)}, u32[]{:S(2)}) copy-start(bf16[1024,384]{1,0:T(8,128)(2,1)} %param.14) | copy-start | bytes 2359300
  0.6 18.8 %collective-permute-start.2 = (bf16[384,192]{0,1:T(8,128)(2,1)}, bf16[384,192]{0,1:T(8,128)(2,1)S(1)}, u32[]{:S(2)}, u32[]{:S(2)}) collective-permute-start(bf16[384,192]{0,1:T(8,128)(2,1)} %param.16), channel_id=1, source_target_pairs={{0,3},{1,0},{2,1},{3,2},{4,7},{5,4},{6,5},{7,6},{8,11},{9,8},{10,9... | collective-permute-start | bytes 442376 | tf_op jit(solution)/shard_map/ppermute | solution.py:31
  3.1 16.4 %collective-permute-start = (bf16[384,192]{0,1:T(8,128)(2,1)}, bf16[384,192]{0,1:T(8,128)(2,1)S(1)}, u32[]{:S(2)}, u32[]{:S(2)}) collective-permute-start(bf16[384,192]{0,1:T(8,128)(2,1)} %param.16), channel_id=1, source_target_pairs={{0,1},{1,2},{2,3},{3,0},{4,5},{5,6},{6,7},{7,4},{8,9},{9,10},{10,1... | collective-permute-start | bytes 442376 | tf_op jit(solution)/shard_map/ppermute | solution.py:31
  3.1 16.6 %collective-permute-start.1 = (bf16[384,192]{0,1:T(8,128)(2,1)}, bf16[384,192]{0,1:T(8,128)(2,1)S(1)}, u32[]{:S(2)}, u32[]{:S(2)}) collective-permute-start(bf16[384,192]{0,1:T(8,128)(2,1)} %param.16), channel_id=1, source_target_pairs={{0,2},{1,3},{2,0},{3,1},{4,6},{5,7},{6,4},{7,5},{8,10},{9,11},{10,... | collective-permute-start | bytes 442376 | tf_op jit(solution)/shard_map/ppermute | solution.py:31
  4.9 1.1 copy-start.11
  6.0 0.8 copy-start.6
  6.0 0.8 copy-start.9
  6.9 6.7 %copy-start.1 = (bf16[48,1024]{1,0:T(8,128)(2,1)S(1)}, bf16[48,1024]{1,0:T(8,128)(2,1)}, u32[]{:S(2)}) copy-start(bf16[48,1024]{1,0:T(8,128)(2,1)} %param.17) | copy-start | bytes 294916
  6.9 6.8 %copy-start.2 = (bf16[384,192]{0,1:T(8,128)(2,1)S(1)}, bf16[384,192]{0,1:T(8,128)(2,1)}, u32[]{:S(2)}) copy-start(bf16[384,192]{0,1:T(8,128)(2,1)} %param.16) | copy-start | bytes 442372
  8.2 13.6 %all-to-all-start = ((f32[32,8,128]{2,1,0:T(8,128)}), f32[32,8,128]{2,1,0:T(8,128)S(1)}, u32[]{:S(2)}, u32[]{:S(2)}) async-start(f32[32,8,128]{2,1,0:T(8,128)} %bitcast.5), calls=%async_computation | async-start | bytes 262144 | tf_op jit(solution)/shard_map/all_to_all | solution.py:59
  22.4 6.2 %copy-start.3 = (bf16[384,192]{0,1:T(8,128)(2,1)S(1)}, bf16[384,192]{0,1:T(8,128)(2,1)}, u32[]{:S(2)}) copy-start(bf16[384,192]{0,1:T(8,128)(2,1)} %param.15) | copy-start | bytes 442372
  24.7 10.6 %all-to-all-start.1 = ((f32[8,8,128]{2,1,0:T(8,128)}), f32[8,8,128]{2,1,0:T(8,128)S(1)}, u32[]{:S(2)}, u32[]{:S(2)}) async-start(f32[8,8,128]{2,1,0:T(8,128)} %select_maximum_fusion.6), calls=%async_computation.1 | async-start | bytes 65536 | tf_op jit(solution)/shard_map/all_to_all | solution.py:86
  28.6 11.4 %collective-permute-start.5 = (bf16[384,192]{0,1:T(8,128)(2,1)S(1)}, bf16[384,192]{0,1:T(8,128)(2,1)S(1)}, u32[]{:S(2)}, u32[]{:S(2)}) collective-permute-start(bf16[384,192]{0,1:T(8,128)(2,1)S(1)} %copy-done.3), channel_id=1, source_target_pairs={{0,3},{1,0},{2,1},{3,2},{4,7},{5,4},{6,5},{7,6},{8,11},{9,8},{10,9... | collective-permute-start | bytes 442376 | tf_op jit(solution)/shard_map/ppermute | solution.py:31
  29.7 10.4 %collective-permute-start.3 = (bf16[384,192]{0,1:T(8,128)(2,1)S(1)}, bf16[384,192]{0,1:T(8,128)(2,1)}, u32[]{:S(2)}, u32[]{:S(2)}) collective-permute-start(bf16[384,192]{0,1:T(8,128)(2,1)S(1)} %copy-done.3), channel_id=1, source_target_pairs={{0,1},{1,2},{2,3},{3,0},{4,5},{5,6},{6,7},{7,4},{8,9},{9,10},{10,1... | collective-permute-start | bytes 442376 | tf_op jit(solution)/shard_map/ppermute | solution.py:31
  29.7 11.5 %collective-permute-start.4 = (bf16[384,192]{0,1:T(8,128)(2,1)S(1)}, bf16[384,192]{0,1:T(8,128)(2,1)}, u32[]{:S(2)}, u32[]{:S(2)}) collective-permute-start(bf16[384,192]{0,1:T(8,128)(2,1)S(1)} %copy-done.3), channel_id=1, source_target_pairs={{0,2},{1,3},{2,0},{3,1},{4,6},{5,7},{6,4},{7,5},{8,10},{9,11},{10,... | collective-permute-start | bytes 442376 | tf_op jit(solution)/shard_map/ppermute | solution.py:31
  35.3 1.1 copy-start.8
  37.2 10.8 %all-to-all-start.2 = ((f32[32,8,128]{2,1,0:T(8,128)}), f32[32,8,128]{2,1,0:T(8,128)S(1)}, u32[]{:S(2)}, u32[]{:S(2)}) async-start(f32[32,8,128]{2,1,0:T(8,128)} %bitcast.26), calls=%async_computation.2 | async-start | bytes 262144 | tf_op jit(solution)/shard_map/all_to_all | solution.py:59
  48.7 13.7 %copy-start.7 = (f32[8,1024]{1,0:T(8,128)S(1)}, f32[8,1024]{1,0:T(8,128)}, u32[]{:S(2)}) copy-start(f32[8,1024]{1,0:T(8,128)} %param.10) | copy-start | bytes 98308
  50.9 10.0 %all-to-all-start.3 = ((f32[8,8,128]{2,1,0:T(8,128)}), f32[8,8,128]{2,1,0:T(8,128)S(1)}, u32[]{:S(2)}, u32[]{:S(2)}) async-start(f32[8,8,128]{2,1,0:T(8,128)} %select_maximum_fusion.4), calls=%async_computation.3 | async-start | bytes 65536 | tf_op jit(solution)/shard_map/all_to_all | solution.py:86
  63.5 1.3 %copy-start.4 = (f32[8,1024]{1,0:T(8,128)}, f32[8,1024]{1,0:T(8,128)S(1)}, u32[]{:S(2)}) copy-start(f32[8,1024]{1,0:T(8,128)S(1)} %get-tuple-element.18) | copy-start | bytes 98308
  75.4 12.4 %copy-start.10 = (f32[8]{0:T(128)S(1)}, f32[8]{0:T(128)}, u32[]{:S(2)}) copy-start(f32[8]{0:T(128)} %get-tuple-element.6) | copy-start | bytes 100
  75.4 12.4 %copy-start.5 = (f32[8,1024]{1,0:T(8,128)S(1)}, f32[8,1024]{1,0:T(8,128)}, u32[]{:S(2)}) copy-start(f32[8,1024]{1,0:T(8,128)} %copy-done.4) | copy-start | bytes 98308
  77.6 10.0 %all-to-all-start.5 = ((f32[8,8,128]{2,1,0:T(8,128)}), f32[8,8,128]{2,1,0:T(8,128)S(1)}, u32[]{:S(2)}, u32[]{:S(2)}) async-start(f32[8,8,128]{2,1,0:T(8,128)} %select_maximum_fusion.2), calls=%async_computation.5 | async-start | bytes 65536 | tf_op jit(solution)/shard_map/all_to_all | solution.py:86
  101.8 10.0 %all-to-all-start.7 = ((f32[8,8,128]{2,1,0:T(8,128)}), f32[8,8,128]{2,1,0:T(8,128)S(1)}, u32[]{:S(2)}, u32[]{:S(2)}) async-start(f32[8,8,128]{2,1,0:T(8,128)} %select_maximum_fusion), calls=%async_computation.7 | async-start | bytes 65536 | tf_op jit(solution)/shard_map/all_to_all | solution.py:86

commit v2 on v0

v2 whole, which is shorter than its diff:
```python
import jax
import jax.numpy as jnp
from jax import lax
from jax.experimental import pallas as pl
from jax.experimental.pallas import tpu as pltpu
from jax.sharding import PartitionSpec as P

ITERS = 2
LANES = 128
F32 = jnp.float32
BF16 = jnp.bfloat16
VMEM = pl.BlockSpec(memory_space=pltpu.VMEM)
SMEM = pl.BlockSpec(memory_space=pltpu.SMEM)
TRANSPOSED = (((1,), (1,)), ((), ()))


def call(body, args, out_shape, scalars=0):
    specs = [SMEM] * scalars + [VMEM] * (len(args) - scalars)
    return pl.pallas_call(
        body,
        in_specs=specs,
        out_specs=jax.tree.map(lambda _: VMEM, out_shape),
        out_shape=out_shape,
    )(*args)


def dot_lanes(value, spare):
    high = value.astype(BF16).astype(F32)
    middle = (value - high).astype(BF16).astype(F32)
    low = value - high - middle
    lane = lax.broadcasted_iota(jnp.int32, (value.shape[0], spare), 1)
    parts = jnp.where(lane == 0, high, jnp.where(lane == 1, middle, 0.0))
    return jnp.where(lane == 2, low, parts)


def pack(values, index, rank_size, extras):
    piece = values[:, index * rank_size : (index + 1) * rank_size]
    return jnp.concatenate([piece, extras], axis=1).astype(BF16)


def unpack(blocks, rank_size):
    wide = [block.astype(F32) for block in blocks]
    carried = wide[0]
    for block in wide[1:]:
        carried = carried + block
    joined = jnp.concatenate([block[:, :rank_size] for block in wide], axis=1).astype(BF16)
    lane = lax.broadcasted_iota(jnp.int32, carried.shape, 1)
    carried = jnp.where((lane >= rank_size) & (lane < rank_size + 3), carried, 0.0)
    return joined, jnp.sum(carried, axis=1, keepdims=True)


def middle_stage(sources, incoming, gram_high, gram_low, pieces, rank_size):
    leaves, row_count, sides, width = incoming.shape

    def body(sources_ref, incoming_ref, high_ref, low_ref, *refs):
        piece_refs = refs[:row_count]
        out_ref, total_ref = refs[row_count:]
        totals = 0.0
        carried = 0.0
        for shift in range(row_count):
            source = sources_ref[shift]
            blocks = [incoming_ref[leaf, source] for leaf in range(leaves)]
            joined, dots = unpack(blocks, rank_size)
            carried = carried + dots
            totals = totals + jnp.dot(
                joined, piece_refs[shift][...], preferred_element_type=F32
            )
        head_coef = totals.astype(BF16)
        gathered = jnp.dot(head_coef, high_ref[...], preferred_element_type=F32)
        gathered = gathered + jnp.dot(head_coef, low_ref[...], preferred_element_type=F32)
        returned = lax.dot_general(
            gathered.astype(BF16), piece_refs[0][...], TRANSPOSED, preferred_element_type=F32
        )
        own_dot = jnp.sum(head_coef.astype(F32) * gathered, axis=1, keepdims=True)
        extras = dot_lanes(own_dot, width - rank_size)
        for leaf in range(leaves):
            out_ref[leaf] = pack(returned, leaf, rank_size, extras)
        total_ref[...] = jnp.broadcast_to(carried, (sides, LANES))

    return call(
        body,
        (sources, incoming, gram_high, gram_low, *pieces),
        (
            jax.ShapeDtypeStruct((leaves, sides, width), BF16),
            jax.ShapeDtypeStruct((sides, LANES), F32),
        ),
        scalars=1,
    )


def block_stage(update, state, columns, diagonal, arrived, local_total, sizes, send, keep):
    leaves, row_count, sides, points, rank_size, width = sizes
    returns = arrived is not None
    kept = [
        jax.ShapeDtypeStruct((sides, points if full else LANES), F32) for full in keep
    ]
    sent = [jax.ShapeDtypeStruct((leaves, row_count, sides, width), BF16)] if send else []
    args = [columns, diagonal[None, :]] + ([arrived, local_total] if returns else [])
    first = len(args)
    args += state

    def body(*refs):
        outs = refs[len(args) :]
        columns_ref, diagonal_ref = refs[:2]
        image = total = None
        if returns:
            joined, dots = unpack([refs[2][leaf] for leaf in range(leaves)], rank_size)
            total = refs[3][:, :1] + dots
            image = lax.dot_general(
                joined, columns_ref[...], TRANSPOSED, preferred_element_type=F32
            )
        values = [ref[...] for ref in refs[first : len(args)]]
        results, field, scaled = update(image, total, diagonal_ref[...], *values)
        for ref, value in zip(outs, results):
            ref[...] = jnp.broadcast_to(value, ref.shape)
        if send:
            coeffs = jnp.dot(field.astype(BF16), columns_ref[...], preferred_element_type=F32)
            own_dot = jnp.sum(field * scaled, axis=1, keepdims=True)
            extras = dot_lanes(own_dot, width - rank_size)
            for leaf in range(leaves):
                chunk = pack(coeffs, leaf, rank_size, extras)
                for row in range(row_count):
                    outs[len(kept)][leaf, row] = chunk

    return call(body, args, tuple(kept + sent))


def start_step(image, total, diagonal, right_side):
    return (), right_side, right_side / diagonal


def first_direction(image, total, diagonal, residual):
    direction = residual / diagonal + image
    return (direction, total), direction, direction * diagonal


def advance(image, total, diagonal, direction, residual, solution, residual_dot):
    image = direction * diagonal + image
    alpha_step = residual_dot[:, :1] / total
    solution = solution + alpha_step * direction
    residual = residual - alpha_step * image
    return (solution, residual), residual, residual / diagonal


def next_direction(image, total, diagonal, direction, residual, residual_dot):
    precond = residual / diagonal + image
    direction = precond + (total / residual_dot[:, :1]) * direction
    return (direction, total), direction, direction * diagonal


def per_device(
    right_side, diagonal, tree_order, mid_perm, col_factor, mid_factor, pre_factor, row_factor
):
    sides, points = right_side.shape
    rank_size = row_factor.shape[0]
    leaves = mid_perm.shape[0]
    row_count = mid_factor.shape[1] // rank_size
    width = -(-(rank_size + 3) // LANES) * LANES
    row = lax.axis_index("rows")
    shifts = jnp.arange(row_count, dtype=jnp.int32)
    sources = (row - shifts) % row_count

    def gather_rows(block):
        pieces = [block]
        for shift in range(1, row_count):
            ring = [(i, (i + shift) % row_count) for i in range(row_count)]
            pieces.append(lax.ppermute(block, "rows", ring))
        return pieces

    own_gram = jnp.dot(row_factor, row_factor.T, preferred_element_type=F32)
    gram_pieces = jnp.stack(gather_rows(own_gram))
    pre_pieces = gather_rows(pre_factor)
    mid_pieces = gather_rows(mid_factor)
    grams = jnp.take(gram_pieces, (row - shifts) % row_count, axis=0)
    same = (shifts[:, None] == shifts[None, :]).astype(F32)
    gram = grams[:, :, None, :] * same[:, None, :, None]
    gram = gram.reshape(row_count * rank_size, row_count * rank_size)
    gram_high = lax.reduce_precision(gram, 8, 7)
    gram_low = (gram - gram_high).astype(BF16)
    gram_high = gram_high.astype(BF16)

    local_index = tree_order % points
    point_ids = jnp.arange(points, dtype=jnp.int32)
    place = (point_ids[:, None] == local_index[None, :]).astype(BF16)
    columns = jnp.dot(place, col_factor, preferred_element_type=F32).astype(BF16)
    slots = (mid_perm[:, None] * rank_size + jnp.arange(rank_size)[None, :]).reshape(-1)
    column_ids = jnp.arange(leaves * rank_size, dtype=jnp.int32)
    move = (column_ids[:, None] == slots[None, :]).astype(BF16)
    columns = jnp.dot(columns, move, preferred_element_type=F32).astype(BF16)
    sizes = (leaves, row_count, sides, points, rank_size, width)

    def exchange(outgoing, pieces):
        incoming = lax.all_to_all(
            outgoing.reshape(leaves * row_count, sides, width),
            ("leaf", "rows"),
            split_axis=0,
            concat_axis=0,
            tiled=True,
        )
        incoming = incoming.reshape(leaves, row_count, sides, width)
        returned, local_total = middle_stage(
            sources, incoming, gram_high, gram_low, pieces, rank_size
        )
        arrived = lax.all_to_all(returned, "leaf", split_axis=0, concat_axis=0, tiled=True)
        return arrived, local_total

    def stage(update, state, received, send, keep):
        return block_stage(update, state, columns, diagonal, *received, sizes, send, keep)

    (outgoing,) = stage(start_step, [right_side], (None, None), True, ())
    received = exchange(outgoing, pre_pieces)
    direction, residual_dot, outgoing = stage(
        first_direction, [right_side], received, True, (True, False)
    )
    solution = jnp.zeros_like(right_side)
    residual = right_side
    for iteration in range(ITERS):
        received = exchange(outgoing, mid_pieces)
        more = iteration + 1 < ITERS
        state = [direction, residual, solution, residual_dot]
        solution, residual, *sent = stage(advance, state, received, more, (True, True))
        if more:
            received = exchange(sent[0], pre_pieces)
            state = [direction, residual, residual_dot]
            direction, residual_dot, outgoing = stage(
                next_direction, state, received, True, (True, False)
            )
    return (solution, residual)


def solution(mesh):
    return jax.shard_map(
        per_device,
        mesh=mesh,
        in_specs=(
            P(None, ("leaf", "rows")),
            P(("leaf", "rows")),
            P(("leaf", "rows")),
            P(),
            P(("leaf", "rows"), None),
            P("leaf", "rows"),
            P("leaf", "rows"),
            P(None, ("leaf", "rows")),
        ),
        out_specs=(P(None, ("leaf", "rows")), P(None, ("leaf", "rows"))),
        check_vma=False,
    )
```

time: 277 us -> 124 us (0.45)
  blocking collectives: 205 us -> 52.8 us
  local copies, waits for them, and re-layouts: 37.2 us -> 4.68 us
  Pallas kernels: 0 us -> 21.8 us
  waiting for transfers between devices: 7.17 us -> 16.8 us
  starting transfers between devices: 10.6 us -> 19.9 us
  other arithmetic: 7.88 us -> 2.93 us
    psum x7 -> x0, blocking collectives: 139 us -> none  [the longest x2 76.4 us: precond_norm(): return lax.psum(jnp.sum(first * second, axis=1), ('leaf', 'rows'))]
    pallas_call x0 -> x9, Pallas kernels: none -> 21.8 us  [call(): pl.pallas_call(body, in_specs=specs, out_specs=jax.tree.map(lambda _: VME...]
    scatter x8 -> x0, local copies, waits for them, and re-layouts: 13.7 us -> none  [gram_apply(): return jnp.zeros_like(tree_out).at[:, local_index].set(tree_out)]
    gather x8 -> x1, local copies, waits for them, and re-layouts: 13.3 us -> 0.56 us  [per_device(): grams = jnp.take(gram_pieces, (row - shifts) % row_count, axis=0)]
    all_to_all x2 -> x3, waiting for transfers between devices: 7.17 us -> 16.8 us  [the longest x2 12.1 us: exchange(): lax.all_to_all(outgoing.reshape(leaves * row_count, sides, width), ('leaf...]
    ppermute x0 -> x9, starting transfers between devices: none -> 8.34 us  [gather_rows(): pieces.append(lax.ppermute(block, 'rows', ring))]
    all_to_all x6 -> x5, blocking collectives: 60.9 us -> 52.8 us  [the longest x3 31.5 us: exchange(): lax.all_to_all(returned, 'leaf', split_axis=0, concat_axis=0, tiled=True)]
    all_to_all x16 -> x0, other arithmetic: 5.83 us -> none  [the longest x8 2.92 us: gram_apply(): lax.all_to_all(returned.reshape(leaves, sides * rank_size), 'leaf', split...]
  transfers between devices with their start and end apart: 2 -> 12, of which waited for: 2 -> 3; matrix products, arithmetic and copies ran while one was open for 0% -> 6% of each run, Pallas kernels for 0% -> 4%
where the time goes in v2:
time: 124 us
  blocking collectives  52.8 us (43%)
  Pallas kernels  21.8 us (18%)
  starting transfers between devices  19.9 us (16%)
  waiting for transfers between devices  16.8 us (14%)
  local copies, waits for them, and re-layouts  4.68 us (4%)
  matrix products  3.8 us (3%)
  other arithmetic  2.93 us (2%)
    all_to_all x3, blocking collectives, exchange(): lax.all_to_all(returned, 'leaf', split_axis=0, concat_axis=0, tiled=True)  31.5 us
    pallas_call x9, Pallas kernels, call(): pl.pallas_call(body, in_specs=specs, out_specs=jax.tree.map(lambda _: VME...  21.8 us
    all_to_all x2, blocking collectives, exchange(): lax.all_to_all(outgoing.reshape(leaves * row_count, sides, width), ('leaf...  21.3 us
    all_to_all x2, waiting for transfers between devices, exchange(): lax.all_to_all(outgoing.reshape(leaves * row_count, sides, width), ('leaf...  12.1 us
    ppermute x9, starting transfers between devices, gather_rows(): pieces.append(lax.ppermute(block, 'rows', ring))  8.34 us
    all_to_all x2, starting transfers between devices, exchange(): lax.all_to_all(outgoing.reshape(leaves * row_count, sides, width), ('leaf...  7.52 us
    all_to_all x1, waiting for transfers between devices, exchange(): lax.all_to_all(returned, 'leaf', split_axis=0, concat_axis=0, tiled=True)  4.68 us
    all_to_all x1, starting transfers between devices, exchange(): lax.all_to_all(returned, 'leaf', split_axis=0, concat_axis=0, tiled=True)  4.04 us
  transfers between devices with their start and end apart: 12, of which 3 were waited for; matrix products, arithmetic and copies ran while one was open for 6% of the time, Pallas kernels for 4%

profile of v2, /device:TPU:0, one launch (start us, length us, event | category | flops | bytes accessed | tf_op | source)
XLA Modules:
  0.0 123.7 jit_solution(2348732399865544760)
XLA Ops:
  0.6 0.0 copy-start
  0.6 1.2 fusion.10
  1.8 2.5 %collective-permute-start.2 = (f32[48,48]{1,0:T(8,128)S(1)}, f32[48,48]{1,0:T(8,128)S(1)}, u32[]{:S(2)}, u32[]{:S(2)}) collective-permute-start(f32[48,48]{1,0:T(8,128)S(1)} %fusion.10), channel_id=1, source_target_pairs={{0,3},{1,0},{2,1},{3,2},{4,7},{5,4},{6,5},{7,6},{8,11},{9,8},{10,9... | collective-permute-start | bytes 27656 | tf_op jit(solution)/shard_map/ppermute | solution.py:167
  4.3 0.6 collective-permute-start.1
  4.9 0.2 collective-permute-start
  5.1 1.0 copy.13.refs_0_
  6.1 0.0 copy-start.1
  6.2 1.6 %collective-permute-start.5 = (bf16[384,192]{1,0:T(8,128)(2,1)S(1)}, bf16[384,192]{1,0:T(8,128)(2,1)S(1)}, u32[]{:S(2)}, u32[]{:S(2)}) collective-permute-start(bf16[384,192]{1,0:T(8,128)(2,1)S(1)} %copy.13.refs_0_), channel_id=1, source_target_pairs={{0,3},{1,0},{2,1},{3,2},{4,7},{5,4},{6,5},{7,6},{8,11},{9,8},{10,9... | collective-permute-start | bytes 442376 | tf_op jit(solution)/shard_map/ppermute | solution.py:167
  7.8 1.4 %collective-permute-start.4 = (bf16[384,192]{1,0:T(8,128)(2,1)S(1)}, bf16[384,192]{1,0:T(8,128)(2,1)S(1)}, u32[]{:S(2)}, u32[]{:S(2)}) collective-permute-start(bf16[384,192]{1,0:T(8,128)(2,1)S(1)} %copy.13.refs_0_), channel_id=1, source_target_pairs={{0,2},{1,3},{2,0},{3,1},{4,6},{5,7},{6,4},{7,5},{8,10},{9,11},{10,... | collective-permute-start | bytes 442376 | tf_op jit(solution)/shard_map/ppermute | solution.py:167
  9.2 0.7 broadcast_multiply_fusion.1
  9.8 0.1 iota_add_fusion
  9.9 0.1 add.64
  10.0 0.7 add_select_fusion
  10.7 2.6 %convolution_convert_fusion.refs_0_ = bf16[1024,384]{1,0:T(8,128)(2,1)} fusion(bf16[1024,384]{1,0:T(8,128)(2,1)S(1)} %copy-done, s32[1024]{0:T(1024)S(1)} %add_select_fusion, s32[384]{0:T(512)S(1)} %add.64), kind=kOutput, calls=%fused_computation.5 | convolution fusion | flops 1109278720 | bytes 1578496 | tf_op jit(solution)/shard_map/dot_general | solution.py:189
  13.3 2.1 %shard_map.95 = bf16[8,4,8,128]{3,2,1,0:T(8,128)(2,1)} custom-call(bf16[1024,384]{1,0:T(8,128)(2,1)} %convolution_convert_fusion.refs_0_, f32[1,1024]{1,0:T(1,128)} %bitcast.23, f32[8,1024]{1,0:T(8,128)} %refs_5_.1), custom_call_target="tpu_custom_call" | custom-call | tf_op jit(solution)/shard_map/pallas_call | solution.py:19
  15.4 5.0 %all-to-all-start = ((bf16[32,8,128]{2,1,0:T(8,128)(2,1)}), bf16[32,8,128]{2,1,0:T(8,128)(2,1)S(1)}, u32[]{:S(2)}, u32[]{:S(2)}) async-start(bf16[32,8,128]{2,1,0:T(8,128)(2,1)} %bitcast.18), calls=%async_computation | async-start | bytes 131072 | tf_op jit(solution)/shard_map/all_to_all | solution.py:193
  20.4 0.5 and_select_fusion.1.sources_ref
  21.0 0.0 collective-permute-done.2
  21.0 0.3 collective-permute-start.3
  21.3 0.0 collective-permute-done.1
  21.3 0.0 collective-permute-done
  21.3 0.6 gather_fusion
  21.9 0.1 broadcast_select_fusion
  22.0 0.1 broadcast_multiply_fusion
  22.1 0.2 mul.25
  22.3 0.7 fusion.4
  23.0 4.8 %all-to-all-done = bf16[32,8,128]{2,1,0:T(8,128)(2,1)S(1)} async-done(((bf16[32,8,128]{2,1,0:T(8,128)(2,1)}), bf16[32,8,128]{2,1,0:T(8,128)(2,1)S(1)}, u32[]{:S(2)}, u32[]{:S(2)}) %all-to-all-start) | async-done | bytes 65568 | tf_op jit(solution)/shard_map/all_to_all | solution.py:193
  27.8 0.0 collective-permute-done.5.refs_3_
  27.8 0.0 collective-permute-done.4.refs_2_
  27.8 0.0 collective-permute-done.3.refs_1_
  27.8 0.0 copy-start.5
  27.8 0.6 copy-done.9
  28.4 0.1 copy-done.3
  28.5 0.1 copy-done.4
  28.6 0.1 copy-done.5
  28.6 2.6 %shard_map.96 = (bf16[8,8,128]{2,1,0:T(8,128)(2,1)}, f32[8,128]{1,0:T(8,128)}) custom-call(s32[4]{0:T(128)} %and_select_fusion.1.sources_ref, bf16[8,4,8,128]{3,2,1,0:T(8,128)(2,1)} %bitcast.19, bf16[192,192]{1,0:T(8,128)(2,1)} %get-tuple-element.37.high_ref, bf16[192,192]{1,0:T(8,128)(2,1)} %get-tuple-element.36.low_ref, bf16[384,192]{1,0:T(8,128)(2,1)} %copy-done.1, ...), custom_call_target="tpu_custom_call" | custom-call | tf_op jit(solution)/shard_map/pallas_call | solution.py:19
  31.2 4.0 %all-to-all-start.1 = ((bf16[8,8,128]{2,1,0:T(8,128)(2,1)}), bf16[8,8,128]{2,1,0:T(8,128)(2,1)S(1)}, u32[]{:S(2)}, u32[]{:S(2)}) async-start(bf16[8,8,128]{2,1,0:T(8,128)(2,1)} %get-tuple-element.19), calls=%async_computation.1 | async-start | bytes 32768 | tf_op jit(solution)/shard_map/all_to_all | solution.py:204
  35.3 0.0 copy-done.11
  35.3 0.1 copy.17.refs_0_
  35.4 0.0 copy-start.2
  35.5 0.1 collective-permute-start.8
  35.5 1.5 %collective-permute-start.7 = (bf16[384,192]{1,0:T(8,128)(2,1)S(1)}, bf16[384,192]{1,0:T(8,128)(2,1)S(1)}, u32[]{:S(2)}, u32[]{:S(2)}) collective-permute-start(bf16[384,192]{1,0:T(8,128)(2,1)S(1)} %copy.17.refs_0_), channel_id=1, source_target_pairs={{0,2},{1,3},{2,0},{3,1},{4,6},{5,7},{6,4},{7,5},{8,10},{9,11},{10,... | collective-permute-start | bytes 442376 | tf_op jit(solution)/shard_map/ppermute | solution.py:167
  37.0 0.2 collective-permute-start.6
  37.2 4.7 %all-to-all-done.1.refs_2_ = bf16[8,8,128]{2,1,0:T(8,128)(2,1)S(1)} async-done(((bf16[8,8,128]{2,1,0:T(8,128)(2,1)}), bf16[8,8,128]{2,1,0:T(8,128)(2,1)S(1)}, u32[]{:S(2)}, u32[]{:S(2)}) %all-to-all-start.1) | async-done | bytes 16416 | tf_op jit(solution)/shard_map/all_to_all | solution.py:204
  41.9 0.6 copy-done.12
  42.5 2.4 %shard_map.97 = (f32[8,1024]{1,0:T(8,128)}, f32[8,128]{1,0:T(8,128)}, bf16[8,4,8,128]{3,2,1,0:T(8,128)(2,1)}) custom-call(bf16[1024,384]{1,0:T(8,128)(2,1)} %convolution_convert_fusion.refs_0_, f32[1,1024]{1,0:T(1,128)} %bitcast.24, bf16[8,8,128]{2,1,0:T(8,128)(2,1)} %copy-done.12, f32[8,128]{1,0:T(8,128)} %get-tuple-element.20.refs_3_, f32[8,1024]{1,0:T(8,128)} %refs_5_.1), custom_call_target="tpu_custom_call" | custom-call | tf_op jit(solution)/shard_map/pallas_call | solution.py:19
  44.8 2.6 %all-to-all-start.2 = ((bf16[32,8,128]{2,1,0:T(8,128)(2,1)}), bf16[32,8,128]{2,1,0:T(8,128)(2,1)S(1)}, u32[]{:S(2)}, u32[]{:S(2)}) async-start(bf16[32,8,128]{2,1,0:T(8,128)(2,1)} %bitcast.29), calls=%async_computation.2 | async-start | bytes 131072 | tf_op jit(solution)/shard_map/all_to_all | solution.py:193
  47.4 0.0 collective-permute-done.8.refs_3_
  47.4 0.0 collective-permute-done.7.refs_2_
  47.4 0.0 collective-permute-done.6.refs_1_
  47.5 7.3 %all-to-all-done.2 = bf16[32,8,128]{2,1,0:T(8,128)(2,1)S(1)} async-done(((bf16[32,8,128]{2,1,0:T(8,128)(2,1)}), bf16[32,8,128]{2,1,0:T(8,128)(2,1)S(1)}, u32[]{:S(2)}, u32[]{:S(2)}) %all-to-all-start.2) | async-done | bytes 65568 | tf_op jit(solution)/shard_map/all_to_all | solution.py:193
  54.8 0.6 copy-done.10
  55.4 2.6 %shard_map.98 = (bf16[8,8,128]{2,1,0:T(8,128)(2,1)}, f32[8,128]{1,0:T(8,128)}) custom-call(s32[4]{0:T(128)} %and_select_fusion.1.sources_ref, bf16[8,4,8,128]{3,2,1,0:T(8,128)(2,1)} %bitcast.20, bf16[192,192]{1,0:T(8,128)(2,1)} %get-tuple-element.37.high_ref, bf16[192,192]{1,0:T(8,128)(2,1)} %get-tuple-element.36.low_ref, bf16[384,192]{1,0:T(8,128)(2,1)} %copy-done.2, ...), custom_call_target="tpu_custom_call" | custom-call | tf_op jit(solution)/shard_map/pallas_call | solution.py:19
  58.0 10.5 %all_to_all.40.refs_2_ = bf16[8,8,128]{2,1,0:T(8,128)(2,1)} all-to-all(bf16[8,8,128]{2,1,0:T(8,128)(2,1)} %get-tuple-element.22), channel_id=1, replica_groups=mesh['leaf'=8,'rows'=4] {'leaf'}, dimensions={0} | all-to-all | bytes 32768 | tf_op jit(solution)/shard_map/all_to_all | solution.py:204
  68.5 0.6 broadcast_in_dim.17.refs_6_
  69.2 2.4 %shard_map.99 = (f32[8,1024]{1,0:T(8,128)}, f32[8,1024]{1,0:T(8,128)}, bf16[8,4,8,128]{3,2,1,0:T(8,128)(2,1)}) custom-call(bf16[1024,384]{1,0:T(8,128)(2,1)} %convolution_convert_fusion.refs_0_, f32[1,1024]{1,0:T(1,128)} %bitcast.25, bf16[8,8,128]{2,1,0:T(8,128)(2,1)} %all_to_all.40.refs_2_, f32[8,128]{1,0:T(8,128)} %get-tuple-element.23.refs_3_, ...), custom_call_target="tpu_custom_call" | custom-call | tf_op jit(solution)/shard_map/pallas_call | solution.py:19
  71.6 10.7 %all_to_all.41 = bf16[32,8,128]{2,1,0:T(8,128)(2,1)} all-to-all(bf16[32,8,128]{2,1,0:T(8,128)(2,1)} %bitcast.31), channel_id=1, replica_groups=mesh['leaf'=8,'rows'=4] {'leaf','rows'}, dimensions={0} | all-to-all | bytes 131072 | tf_op jit(solution)/shard_map/all_to_all | solution.py:193
  82.2 2.6 %shard_map.100 = (bf16[8,8,128]{2,1,0:T(8,128)(2,1)}, f32[8,128]{1,0:T(8,128)}) custom-call(s32[4]{0:T(128)} %and_select_fusion.1.sources_ref, bf16[8,4,8,128]{3,2,1,0:T(8,128)(2,1)} %bitcast.22, bf16[192,192]{1,0:T(8,128)(2,1)} %get-tuple-element.37.high_ref, bf16[192,192]{1,0:T(8,128)(2,1)} %get-tuple-element.36.low_ref, bf16[384,192]{1,0:T(8,128)(2,1)} %copy-done.1, ...), custom_call_target="tpu_custom_call" | custom-call | tf_op jit(solution)/shard_map/pallas_call | solution.py:19
  84.8 10.5 %all_to_all.42.refs_2_ = bf16[8,8,128]{2,1,0:T(8,128)(2,1)} all-to-all(bf16[8,8,128]{2,1,0:T(8,128)(2,1)} %get-tuple-element.27), channel_id=1, replica_groups=mesh['leaf'=8,'rows'=4] {'leaf'}, dimensions={0} | all-to-all | bytes 32768 | tf_op jit(solution)/shard_map/all_to_all | solution.py:204
  95.3 2.4 %shard_map.101 = (f32[8,1024]{1,0:T(8,128)}, f32[8,128]{1,0:T(8,128)}, bf16[8,4,8,128]{3,2,1,0:T(8,128)(2,1)}) custom-call(bf16[1024,384]{1,0:T(8,128)(2,1)} %convolution_convert_fusion.refs_0_, f32[1,1024]{1,0:T(1,128)} %bitcast.26, bf16[8,8,128]{2,1,0:T(8,128)(2,1)} %all_to_all.42.refs_2_, f32[8,128]{1,0:T(8,128)} %get-tuple-element.28.refs_3_, ...), custom_call_target="tpu_custom_call" | custom-call | tf_op jit(solution)/shard_map/pallas_call | solution.py:19
  97.7 10.7 %all_to_all.43 = bf16[32,8,128]{2,1,0:T(8,128)(2,1)} all-to-all(bf16[32,8,128]{2,1,0:T(8,128)(2,1)} %bitcast.30), channel_id=1, replica_groups=mesh['leaf'=8,'rows'=4] {'leaf','rows'}, dimensions={0} | all-to-all | bytes 131072 | tf_op jit(solution)/shard_map/all_to_all | solution.py:193
  108.4 2.6 %shard_map.102 = (bf16[8,8,128]{2,1,0:T(8,128)(2,1)}, f32[8,128]{1,0:T(8,128)}) custom-call(s32[4]{0:T(128)} %and_select_fusion.1.sources_ref, bf16[8,4,8,128]{3,2,1,0:T(8,128)(2,1)} %bitcast.21, bf16[192,192]{1,0:T(8,128)(2,1)} %get-tuple-element.37.high_ref, bf16[192,192]{1,0:T(8,128)(2,1)} %get-tuple-element.36.low_ref, bf16[384,192]{1,0:T(8,128)(2,1)} %copy-done.2, ...), custom_call_target="tpu_custom_call" | custom-call | tf_op jit(solution)/shard_map/pallas_call | solution.py:19
  111.0 10.5 %all_to_all.44.refs_2_ = bf16[8,8,128]{2,1,0:T(8,128)(2,1)} all-to-all(bf16[8,8,128]{2,1,0:T(8,128)(2,1)} %get-tuple-element.31), channel_id=1, replica_groups=mesh['leaf'=8,'rows'=4] {'leaf'}, dimensions={0} | all-to-all | bytes 32768 | tf_op jit(solution)/shard_map/all_to_all | solution.py:204
  121.5 2.2 %shard_map.103 = (f32[8,1024]{1,0:T(8,128)}, f32[8,1024]{1,0:T(8,128)}) custom-call(bf16[1024,384]{1,0:T(8,128)(2,1)} %convolution_convert_fusion.refs_0_, f32[1,1024]{1,0:T(1,128)} %bitcast.27, bf16[8,8,128]{2,1,0:T(8,128)(2,1)} %all_to_all.44.refs_2_, f32[8,128]{1,0:T(8,128)} %get-tuple-element.32.refs_3_, f32[8,1024]{1,0:T(8,128)} %get-tuple-element.33.refs_4_, ...), custom_call_target="tpu_custom_call" | custom-call | tf_op jit(solution)/shard_map/pallas_call | solution.py:19
  (20 shorter events, 0.1 us)
Async XLA Ops:
  0.6 10.1 %copy-start = (bf16[1024,384]{1,0:T(8,128)(2,1)S(1)}, bf16[1024,384]{1,0:T(8,128)(2,1)}, u32[]{:S(2)}) copy-start(bf16[1024,384]{1,0:T(8,128)(2,1)} %param.12) | copy-start | bytes 2359300
  1.8 19.2 %collective-permute-start.2 = (f32[48,48]{1,0:T(8,128)S(1)}, f32[48,48]{1,0:T(8,128)S(1)}, u32[]{:S(2)}, u32[]{:S(2)}) collective-permute-start(f32[48,48]{1,0:T(8,128)S(1)} %fusion.10), channel_id=1, source_target_pairs={{0,3},{1,0},{2,1},{3,2},{4,7},{5,4},{6,5},{7,6},{8,11},{9,8},{10,9... | collective-permute-start | bytes 27656 | tf_op jit(solution)/shard_map/ppermute | solution.py:167
  4.3 17.0 %collective-permute-start.1 = (f32[48,48]{1,0:T(8,128)S(1)}, f32[48,48]{1,0:T(8,128)S(1)}, u32[]{:S(2)}, u32[]{:S(2)}) collective-permute-start(f32[48,48]{1,0:T(8,128)S(1)} %fusion.10), channel_id=1, source_target_pairs={{0,2},{1,3},{2,0},{3,1},{4,6},{5,7},{6,4},{7,5},{8,10},{9,11},{10,... | collective-permute-start | bytes 27656 | tf_op jit(solution)/shard_map/ppermute | solution.py:167
  4.9 16.4 %collective-permute-start = (f32[48,48]{1,0:T(8,128)S(1)}, f32[48,48]{1,0:T(8,128)S(1)}, u32[]{:S(2)}, u32[]{:S(2)}) collective-permute-start(f32[48,48]{1,0:T(8,128)S(1)} %fusion.10), channel_id=1, source_target_pairs={{0,1},{1,2},{2,3},{3,0},{4,5},{5,6},{6,7},{7,4},{8,9},{9,10},{10,1... | collective-permute-start | bytes 27656 | tf_op jit(solution)/shard_map/ppermute | solution.py:167
  6.1 14.8 %copy-start.1 = (bf16[384,192]{1,0:T(8,128)(2,1)}, bf16[384,192]{1,0:T(8,128)(2,1)S(1)}, u32[]{:S(2)}) copy-start(bf16[384,192]{1,0:T(8,128)(2,1)S(1)} %copy.13.refs_0_) | copy-start | bytes 442372
  6.2 21.6 %collective-permute-start.5 = (bf16[384,192]{1,0:T(8,128)(2,1)S(1)}, bf16[384,192]{1,0:T(8,128)(2,1)S(1)}, u32[]{:S(2)}, u32[]{:S(2)}) collective-permute-start(bf16[384,192]{1,0:T(8,128)(2,1)S(1)} %copy.13.refs_0_), channel_id=1, source_target_pairs={{0,3},{1,0},{2,1},{3,2},{4,7},{5,4},{6,5},{7,6},{8,11},{9,8},{10,9... | collective-permute-start | bytes 442376 | tf_op jit(solution)/shard_map/ppermute | solution.py:167
  7.8 20.0 %collective-permute-start.4 = (bf16[384,192]{1,0:T(8,128)(2,1)S(1)}, bf16[384,192]{1,0:T(8,128)(2,1)S(1)}, u32[]{:S(2)}, u32[]{:S(2)}) collective-permute-start(bf16[384,192]{1,0:T(8,128)(2,1)S(1)} %copy.13.refs_0_), channel_id=1, source_target_pairs={{0,2},{1,3},{2,0},{3,1},{4,6},{5,7},{6,4},{7,5},{8,10},{9,11},{10,... | collective-permute-start | bytes 442376 | tf_op jit(solution)/shard_map/ppermute | solution.py:167
  15.4 12.4 %all-to-all-start = ((bf16[32,8,128]{2,1,0:T(8,128)(2,1)}), bf16[32,8,128]{2,1,0:T(8,128)(2,1)S(1)}, u32[]{:S(2)}, u32[]{:S(2)}) async-start(bf16[32,8,128]{2,1,0:T(8,128)(2,1)} %bitcast.18), calls=%async_computation | async-start | bytes 131072 | tf_op jit(solution)/shard_map/all_to_all | solution.py:193
  21.0 6.8 %collective-permute-start.3 = (bf16[384,192]{1,0:T(8,128)(2,1)S(1)}, bf16[384,192]{1,0:T(8,128)(2,1)S(1)}, u32[]{:S(2)}, u32[]{:S(2)}) collective-permute-start(bf16[384,192]{1,0:T(8,128)(2,1)S(1)} %copy.13.refs_0_), channel_id=1, source_target_pairs={{0,1},{1,2},{2,3},{3,0},{4,5},{5,6},{6,7},{7,4},{8,9},{9,10},{10,1... | collective-permute-start | bytes 442376 | tf_op jit(solution)/shard_map/ppermute | solution.py:167
  22.3 13.0 %copy-start.11 = (bf16[384,192]{0,1:T(8,128)(2,1)S(1)}, bf16[384,192]{0,1:T(8,128)(2,1)}, u32[]{:S(2)}) copy-start(bf16[384,192]{0,1:T(8,128)(2,1)} %param.13) | copy-start | bytes 442372
  27.8 0.6 copy-start.9
  27.8 0.7 copy-start.3
  27.8 0.8 copy-start.4
  27.8 0.8 copy-start.5
  31.2 10.6 %all-to-all-start.1 = ((bf16[8,8,128]{2,1,0:T(8,128)(2,1)}), bf16[8,8,128]{2,1,0:T(8,128)(2,1)S(1)}, u32[]{:S(2)}, u32[]{:S(2)}) async-start(bf16[8,8,128]{2,1,0:T(8,128)(2,1)} %get-tuple-element.19), calls=%async_computation.1 | async-start | bytes 32768 | tf_op jit(solution)/shard_map/all_to_all | solution.py:204
  35.4 19.4 %copy-start.2 = (bf16[384,192]{1,0:T(8,128)(2,1)}, bf16[384,192]{1,0:T(8,128)(2,1)S(1)}, u32[]{:S(2)}) copy-start(bf16[384,192]{1,0:T(8,128)(2,1)S(1)} %copy.17.refs_0_) | copy-start | bytes 442372
  35.5 12.0 %collective-permute-start.8 = (bf16[384,192]{1,0:T(8,128)(2,1)S(1)}, bf16[384,192]{1,0:T(8,128)(2,1)S(1)}, u32[]{:S(2)}, u32[]{:S(2)}) collective-permute-start(bf16[384,192]{1,0:T(8,128)(2,1)S(1)} %copy.17.refs_0_), channel_id=1, source_target_pairs={{0,3},{1,0},{2,1},{3,2},{4,7},{5,4},{6,5},{7,6},{8,11},{9,8},{10,9... | collective-permute-start | bytes 442376 | tf_op jit(solution)/shard_map/ppermute | solution.py:167
  35.5 11.9 %collective-permute-start.7 = (bf16[384,192]{1,0:T(8,128)(2,1)S(1)}, bf16[384,192]{1,0:T(8,128)(2,1)S(1)}, u32[]{:S(2)}, u32[]{:S(2)}) collective-permute-start(bf16[384,192]{1,0:T(8,128)(2,1)S(1)} %copy.17.refs_0_), channel_id=1, source_target_pairs={{0,2},{1,3},{2,0},{3,1},{4,6},{5,7},{6,4},{7,5},{8,10},{9,11},{10,... | collective-permute-start | bytes 442376 | tf_op jit(solution)/shard_map/ppermute | solution.py:167
  37.0 10.4 %collective-permute-start.6 = (bf16[384,192]{1,0:T(8,128)(2,1)S(1)}, bf16[384,192]{1,0:T(8,128)(2,1)S(1)}, u32[]{:S(2)}, u32[]{:S(2)}) collective-permute-start(bf16[384,192]{1,0:T(8,128)(2,1)S(1)} %copy.17.refs_0_), channel_id=1, source_target_pairs={{0,1},{1,2},{2,3},{3,0},{4,5},{5,6},{6,7},{7,4},{8,9},{9,10},{10,1... | collective-permute-start | bytes 442376 | tf_op jit(solution)/shard_map/ppermute | solution.py:167
  41.9 0.6 copy-start.12
  44.8 10.0 %all-to-all-start.2 = ((bf16[32,8,128]{2,1,0:T(8,128)(2,1)}), bf16[32,8,128]{2,1,0:T(8,128)(2,1)S(1)}, u32[]{:S(2)}, u32[]{:S(2)}) async-start(bf16[32,8,128]{2,1,0:T(8,128)(2,1)} %bitcast.29), calls=%async_computation.2 | async-start | bytes 131072 | tf_op jit(solution)/shard_map/all_to_all | solution.py:193
  47.4 7.4 %copy-start.6 = (bf16[384,192]{1,0:T(8,128)(2,1)}, bf16[384,192]{1,0:T(8,128)(2,1)S(1)}, u32[]{:S(2)}) copy-start(bf16[384,192]{1,0:T(8,128)(2,1)S(1)} %collective-permute-done.8.refs_3_) | copy-start | bytes 442372
  47.4 7.4 %copy-start.7 = (bf16[384,192]{1,0:T(8,128)(2,1)}, bf16[384,192]{1,0:T(8,128)(2,1)S(1)}, u32[]{:S(2)}) copy-start(bf16[384,192]{1,0:T(8,128)(2,1)S(1)} %collective-permute-done.7.refs_2_) | copy-start | bytes 442372
  47.4 7.4 %copy-start.8 = (bf16[384,192]{1,0:T(8,128)(2,1)}, bf16[384,192]{1,0:T(8,128)(2,1)S(1)}, u32[]{:S(2)}) copy-start(bf16[384,192]{1,0:T(8,128)(2,1)S(1)} %collective-permute-done.6.refs_1_) | copy-start | bytes 442372
  54.8 0.6 copy-start.10

commit v3 on v2

--- a/solution.py
+++ b/solution.py
@@ -7,6 +7,7 @@
 
 ITERS = 2
 LANES = 128
+NEAR_BYTES = 1 << 20
 F32 = jnp.float32
 BF16 = jnp.bfloat16
 VMEM = pl.BlockSpec(memory_space=pltpu.VMEM)
@@ -16,6 +17,12 @@
 
 def call(body, args, out_shape, scalars=0):
     specs = [SMEM] * scalars + [VMEM] * (len(args) - scalars)
+    args = [
+        pltpu.with_memory_space_constraint(arg, pltpu.VMEM)
+        if at >= scalars and arg.size * arg.dtype.itemsize <= NEAR_BYTES
+        else arg
+        for at, arg in enumerate(args)
+    ]
     return pl.pallas_call(
         body,
         in_specs=specs,
@@ -81,8 +88,8 @@
         body,
         (sources, incoming, gram_high, gram_low, *pieces),
         (
-            jax.ShapeDtypeStruct((leaves, sides, width), BF16),
-            jax.ShapeDtypeStruct((sides, LANES), F32),
+            pltpu.VMEM((leaves, sides, width), BF16),
+            pltpu.VMEM((sides, LANES), F32),
         ),
         scalars=1,
     )
@@ -91,10 +98,9 @@
 def block_stage(update, state, columns, diagonal, arrived, local_total, sizes, send, keep):
     leaves, row_count, sides, points, rank_size, width = sizes
     returns = arrived is not None
-    kept = [
-        jax.ShapeDtypeStruct((sides, points if full else LANES), F32) for full in keep
-    ]
-    sent = [jax.ShapeDtypeStruct((leaves, row_count, sides, width), BF16)] if send else []
+    kind = pltpu.VMEM if send else jax.ShapeDtypeStruct
+    kept = [kind((sides, points if full else LANES), F32) for full in keep]
+    sent = [kind((leaves, row_count, sides, width), BF16)] if send else []
     args = [columns, diagonal[None, :]] + ([arrived, local_total] if returns else [])
     first = len(args)
     args += state
@@ -134,10 +140,10 @@
     return (direction, total), direction, direction * diagonal
 
 
-def advance(image, total, diagonal, direction, residual, solution, residual_dot):
+def advance(image, total, diagonal, residual_dot, direction, residual, *solution):
     image = direction * diagonal + image
     alpha_step = residual_dot[:, :1] / total
-    solution = solution + alpha_step * direction
+    solution = sum(solution, alpha_step * direction)
     residual = residual - alpha_step * image
     return (solution, residual), residual, residual / diagonal
 
@@ -168,10 +174,9 @@
         return pieces
 
     own_gram = jnp.dot(row_factor, row_factor.T, preferred_element_type=F32)
-    gram_pieces = jnp.stack(gather_rows(own_gram))
+    grams = lax.all_gather(own_gram[None], "rows", axis=0, tiled=True)
     pre_pieces = gather_rows(pre_factor)
     mid_pieces = gather_rows(mid_factor)
-    grams = jnp.take(gram_pieces, (row - shifts) % row_count, axis=0)
     same = (shifts[:, None] == shifts[None, :]).astype(F32)
     gram = grams[:, :, None, :] * same[:, None, :, None]
     gram = gram.reshape(row_count * rank_size, row_count * rank_size)
@@ -183,10 +188,15 @@
     point_ids = jnp.arange(points, dtype=jnp.int32)
     place = (point_ids[:, None] == local_index[None, :]).astype(BF16)
     columns = jnp.dot(place, col_factor, preferred_element_type=F32).astype(BF16)
-    slots = (mid_perm[:, None] * rank_size + jnp.arange(rank_size)[None, :]).reshape(-1)
-    column_ids = jnp.arange(leaves * rank_size, dtype=jnp.int32)
-    move = (column_ids[:, None] == slots[None, :]).astype(BF16)
-    columns = jnp.dot(columns, move, preferred_element_type=F32).astype(BF16)
+    slot_ids = jnp.arange(leaves, dtype=jnp.int32)
+    onehot = (mid_perm[:, None] == slot_ids[None, :]).astype(BF16)
+    columns = jnp.einsum(
+        "qg,ngk->nqk",
+        onehot,
+        columns.reshape(points, leaves, rank_size),
+        preferred_element_type=F32,
+    ).astype(BF16)
+    columns = columns.reshape(points, leaves * rank_size)
     sizes = (leaves, row_count, sides, points, rank_size, width)
 
     def exchange(outgoing, pieces):
@@ -212,20 +222,21 @@
     direction, residual_dot, outgoing = stage(
         first_direction, [right_side], received, True, (True, False)
     )
-    solution = jnp.zeros_like(right_side)
+    solution = []
     residual = right_side
     for iteration in range(ITERS):
         received = exchange(outgoing, mid_pieces)
         more = iteration + 1 < ITERS
-        state = [direction, residual, solution, residual_dot]
-        solution, residual, *sent = stage(advance, state, received, more, (True, True))
+        state = [residual_dot, direction, residual] + solution
+        outs = stage(advance, state, received, more, (True, True))
+        solution, residual, sent = [outs[0]], outs[1], outs[2:]
         if more:
             received = exchange(sent[0], pre_pieces)
             state = [direction, residual, residual_dot]
             direction, residual_dot, outgoing = stage(
                 next_direction, state, received, True, (True, False)
             )
-    return (solution, residual)
+    return (solution[0], residual)
 
 
 def solution(mesh):

time: 124 us -> 101 us (0.81)
  Pallas kernels: 21.8 us -> 11 us
  waiting for transfers between devices: 16.8 us -> 11.7 us
  blocking collectives: 52.8 us -> 50.6 us
  local copies, waits for them, and re-layouts: 4.68 us -> 2.69 us
  matrix products: 3.8 us -> 1.84 us
  other arithmetic: 2.93 us -> 1.44 us
    pallas_call x9, Pallas kernels: 21.8 us -> 11 us  [call(): pl.pallas_call(body, in_specs=specs, out_specs=jax.tree.map(lambda _: VME...]
    all_gather x0 -> x1, blocking collectives: none -> 5.36 us  [per_device(): grams = lax.all_gather(own_gram[None], 'rows', axis=0, tiled=True)]
    all_to_all x3, blocking collectives: 31.5 us -> 27 us  [exchange(): lax.all_to_all(returned, 'leaf', split_axis=0, concat_axis=0, tiled=True)]
    all_to_all x2, waiting for transfers between devices: 12.1 us -> 8.03 us  [exchange(): lax.all_to_all(outgoing.reshape(leaves * row_count, sides, width), ('leaf...]
    all_to_all x2, blocking collectives: 21.3 us -> 18.2 us  [exchange(): lax.all_to_all(outgoing.reshape(leaves * row_count, sides, width), ('leaf...]
    unnamed x28 -> x26, local copies, waits for them, and re-layouts: 3.22 us -> 1.68 us
    all_to_all x1, waiting for transfers between devices: 4.68 us -> 3.41 us  [exchange(): lax.all_to_all(returned, 'leaf', split_axis=0, concat_axis=0, tiled=True)]
    dot_general x1 -> x2, matrix products: 2.64 us -> 1.71 us  [the longest x1 1.11 us: per_device(): jnp.dot(place, col_factor, preferred_element_type=F32).astype(BF16)]
  transfers between devices with their start and end apart: 12 -> 9, of which waited for: 3 -> 4; matrix products, arithmetic and copies ran while one was open for 6% -> 4% of each run, Pallas kernels for 4% -> 2%
where the time goes in v3:
time: 101 us; the launch traced here: 100 us
  blocking collectives  50.6 us (50%)
  starting transfers between devices  19.9 us (20%)
  waiting for transfers between devices  11.7 us (12%)
  Pallas kernels  11 us (11%)
  local copies, waits for them, and re-layouts  2.69 us (3%)
  matrix products  1.84 us (2%)
  other arithmetic  1.44 us (1%)
    all_to_all x3, blocking collectives, exchange(): lax.all_to_all(returned, 'leaf', split_axis=0, concat_axis=0, tiled=True)  27 us
    all_to_all x2, blocking collectives, exchange(): lax.all_to_all(outgoing.reshape(leaves * row_count, sides, width), ('leaf...  18.2 us
    pallas_call x9, Pallas kernels, call(): pl.pallas_call(body, in_specs=specs, out_specs=jax.tree.map(lambda _: VME...  11 us
    all_to_all x2, waiting for transfers between devices, exchange(): lax.all_to_all(outgoing.reshape(leaves * row_count, sides, width), ('leaf...  8.03 us
    ppermute x6, starting transfers between devices, gather_rows(): pieces.append(lax.ppermute(block, 'rows', ring))  7.53 us
    all_to_all x2, starting transfers between devices, exchange(): lax.all_to_all(outgoing.reshape(leaves * row_count, sides, width), ('leaf...  7.45 us
    all_gather x1, blocking collectives, per_device(): grams = lax.all_gather(own_gram[None], 'rows', axis=0, tiled=True)  5.36 us
    all_to_all x1, starting transfers between devices, exchange(): lax.all_to_all(returned, 'leaf', split_axis=0, concat_axis=0, tiled=True)  4.89 us
  transfers between devices with their start and end apart: 9, of which 4 were waited for; matrix products, arithmetic and copies ran while one was open for 4% of the time, Pallas kernels for 2%

profile of v3, /device:TPU:0, one launch (start us, length us, event | category | flops | bytes accessed | tf_op | source)
XLA Modules:
  0.0 100.0 jit_solution(5404103760960741132)
XLA Ops:
  0.6 0.0 copy-start
  0.6 1.1 %copy.28.refs_0_ = bf16[384,192]{1,0:T(8,128)(2,1)S(1)} copy(bf16[384,192]{0,1:T(8,128)(2,1)} %param.14) | data formatting | bytes 294912 | tf_op args[6]
  1.8 0.5 collective-permute-start
  2.3 2.6 %collective-permute-start.1 = (bf16[384,192]{1,0:T(8,128)(2,1)S(1)}, bf16[384,192]{1,0:T(8,128)(2,1)S(1)}, u32[]{:S(2)}, u32[]{:S(2)}) collective-permute-start(bf16[384,192]{1,0:T(8,128)(2,1)S(1)} %copy.28.refs_0_), channel_id=1, source_target_pairs={{0,2},{1,3},{2,0},{3,1},{4,6},{5,7},{6,4},{7,5},{8,10},{9,11},{10,... | collective-permute-start | bytes 442376 | tf_op jit(solution)/shard_map/ppermute | solution.py:173
  4.9 1.4 %collective-permute-start.2 = (bf16[384,192]{1,0:T(8,128)(2,1)S(1)}, bf16[384,192]{1,0:T(8,128)(2,1)S(1)}, u32[]{:S(2)}, u32[]{:S(2)}) collective-permute-start(bf16[384,192]{1,0:T(8,128)(2,1)S(1)} %copy.28.refs_0_), channel_id=1, source_target_pairs={{0,3},{1,0},{2,1},{3,2},{4,7},{5,4},{6,5},{7,6},{8,11},{9,8},{10,9... | collective-permute-start | bytes 442376 | tf_op jit(solution)/shard_map/ppermute | solution.py:173
  6.3 0.7 add_select_fusion
  7.0 0.0 copy-done
  7.0 1.1 %fusion.2 = bf16[1024,384]{0,1:T(8,128)(2,1)S(1)} fusion(bf16[1024,384]{1,0:T(8,128)(2,1)S(1)} %copy-done, s32[1024]{0:T(1024)S(1)} %add_select_fusion), kind=kOutput, calls=%fused_computation.3 | convolution fusion | flops 806748160 | bytes 1576960 | tf_op jit(solution)/shard_map/dot_general | solution.py:190
  8.1 0.0 copy-done.11
  8.1 0.6 fusion.3
  8.7 0.4 copy.23
  9.2 0.0 copy-start.3
  9.2 0.0 copy-start.6
  9.2 0.4 copy.38.refs_0_
  9.6 0.0 copy-start.9
  9.6 0.4 copy-done.3
  9.9 0.0 copy-done.6
  9.9 0.9 shard_map.95
  10.8 4.9 %all-to-all-start = ((bf16[32,8,128]{2,1,0:T(8,128)(2,1)}), bf16[32,8,128]{2,1,0:T(8,128)(2,1)S(1)}, u32[]{:S(2)}, u32[]{:S(2)}) async-start(bf16[32,8,128]{2,1,0:T(8,128)(2,1)} %bitcast.5), calls=%async_computation | async-start | bytes 131072 | tf_op jit(solution)/shard_map/all_to_all | solution.py:203
  15.8 0.0 copy-done.9
  15.8 0.1 fusion.12
  15.9 5.4 %all-gather = f32[192,48]{1,0:T(8,128)S(1)} all-gather(f32[48,48]{1,0:T(8,128)S(1)} %fusion.12), channel_id=2, replica_groups=mesh['leaf'=8,'rows'=4] {'rows'}, dimensions={0}, use_global_device_ids=true | all-gather | bytes 46080 | tf_op jit(solution)/shard_map/all_gather | solution.py:177
  21.3 0.1 broadcast_multiply_fusion
  21.4 0.2 mul.20
  21.7 0.6 and_select_fusion.sources_ref
  22.2 0.9 all-to-all-done
  23.2 0.0 collective-permute-done.refs_1_
  23.2 0.0 collective-permute-done.1.refs_2_
  23.2 0.0 collective-permute-done.2.refs_3_
  23.2 2.0 %shard_map.96 = (bf16[8,8,128]{2,1,0:T(8,128)(2,1)}, f32[8,128]{1,0:T(8,128)S(1)}) custom-call(s32[4]{0:T(128)} %and_select_fusion.sources_ref, bf16[8,4,8,128]{3,2,1,0:T(8,128)(2,1)S(1)} %bitcast.20, bf16[192,192]{1,0:T(8,128)(2,1)S(1)} %get-tuple-element.37.high_ref, bf16[192,192]{1,0:T(8,128)(2,1)S(1)} %get-tuple-element.36.low_ref, ...), custom_call_target="tpu_custom_call" | custom-call | tf_op jit(solution)/shard_map/pallas_call | solution.py:26
  25.1 4.9 %all-to-all-start.1 = ((bf16[8,8,128]{2,1,0:T(8,128)(2,1)}), bf16[8,8,128]{2,1,0:T(8,128)(2,1)S(1)}, u32[]{:S(2)}, u32[]{:S(2)}) async-start(bf16[8,8,128]{2,1,0:T(8,128)(2,1)} %get-tuple-element.19), calls=%async_computation.1 | async-start | bytes 32768 | tf_op jit(solution)/shard_map/all_to_all | solution.py:214
  30.0 0.0 copy-done.10
  30.0 0.1 copy.33.refs_0_
  30.2 0.1 collective-permute-start.3
  30.3 1.5 %collective-permute-start.4 = (bf16[384,192]{1,0:T(8,128)(2,1)S(1)}, bf16[384,192]{1,0:T(8,128)(2,1)}, u32[]{:S(2)}, u32[]{:S(2)}) collective-permute-start(bf16[384,192]{1,0:T(8,128)(2,1)S(1)} %copy.33.refs_0_), channel_id=1, source_target_pairs={{0,2},{1,3},{2,0},{3,1},{4,6},{5,7},{6,4},{7,5},{8,10},{9,11},{10,... | collective-permute-start | bytes 442376 | tf_op jit(solution)/shard_map/ppermute | solution.py:173
  31.8 1.4 %collective-permute-start.5 = (bf16[384,192]{1,0:T(8,128)(2,1)S(1)}, bf16[384,192]{1,0:T(8,128)(2,1)}, u32[]{:S(2)}, u32[]{:S(2)}) collective-permute-start(bf16[384,192]{1,0:T(8,128)(2,1)S(1)} %copy.33.refs_0_), channel_id=1, source_target_pairs={{0,3},{1,0},{2,1},{3,2},{4,7},{5,4},{6,5},{7,6},{8,11},{9,8},{10,9... | collective-permute-start | bytes 442376 | tf_op jit(solution)/shard_map/ppermute | solution.py:173
  33.2 3.4 %all-to-all-done.1.refs_2_ = bf16[8,8,128]{2,1,0:T(8,128)(2,1)S(1)} async-done(((bf16[8,8,128]{2,1,0:T(8,128)(2,1)}), bf16[8,8,128]{2,1,0:T(8,128)(2,1)S(1)}, u32[]{:S(2)}, u32[]{:S(2)}) %all-to-all-start.1) | async-done | bytes 16416 | tf_op jit(solution)/shard_map/all_to_all | solution.py:214
  36.6 1.2 %shard_map.97 = (f32[8,1024]{1,0:T(8,128)S(1)}, f32[8,128]{1,0:T(8,128)S(1)}, bf16[8,4,8,128]{3,2,1,0:T(8,128)(2,1)}) custom-call(bf16[1024,384]{1,0:T(8,128)(2,1)S(1)} %copy.38.refs_0_, f32[1,1024]{1,0:T(1,128)S(1)} %bitcast.25, bf16[8,8,128]{2,1,0:T(8,128)(2,1)S(1)} %all-to-all-done.1.refs_2_, f32[8,128]{1,0:T(8,128)S(1)} %get-tuple-element.20.refs_3_, ...), custom_call_target="tpu_custom_call" | custom-call | tf_op jit(solution)/shard_map/pallas_call | solution.py:26
  37.8 2.6 %all-to-all-start.2 = ((bf16[32,8,128]{2,1,0:T(8,128)(2,1)}), bf16[32,8,128]{2,1,0:T(8,128)(2,1)S(1)}, u32[]{:S(2)}, u32[]{:S(2)}) async-start(bf16[32,8,128]{2,1,0:T(8,128)(2,1)} %bitcast.8), calls=%async_computation.2 | async-start | bytes 131072 | tf_op jit(solution)/shard_map/all_to_all | solution.py:203
  40.4 0.0 collective-permute-done.3.refs_1_
  40.4 0.0 copy-start.1
  40.4 0.0 collective-permute-done.4.refs_2_
  40.4 0.3 collective-permute-done.5.refs_3_
  40.7 7.1 %all-to-all-done.2 = bf16[32,8,128]{2,1,0:T(8,128)(2,1)S(1)} async-done(((bf16[32,8,128]{2,1,0:T(8,128)(2,1)}), bf16[32,8,128]{2,1,0:T(8,128)(2,1)S(1)}, u32[]{:S(2)}, u32[]{:S(2)}) %all-to-all-start.2) | async-done | bytes 65568 | tf_op jit(solution)/shard_map/all_to_all | solution.py:203
  47.8 1.7 %shard_map.98 = (bf16[8,8,128]{2,1,0:T(8,128)(2,1)S(1)}, f32[8,128]{1,0:T(8,128)S(1)}) custom-call(s32[4]{0:T(128)} %and_select_fusion.sources_ref, bf16[8,4,8,128]{3,2,1,0:T(8,128)(2,1)S(1)} %bitcast.21, bf16[192,192]{1,0:T(8,128)(2,1)S(1)} %get-tuple-element.37.high_ref, bf16[192,192]{1,0:T(8,128)(2,1)S(1)} %get-tuple-element.36.low_ref, ...), custom_call_target="tpu_custom_call" | custom-call | tf_op jit(solution)/shard_map/pallas_call | solution.py:26
  49.5 9.0 %all_to_all.40.refs_2_ = bf16[8,8,128]{2,1,0:T(8,128)(2,1)S(1)} all-to-all(bf16[8,8,128]{2,1,0:T(8,128)(2,1)S(1)} %get-tuple-element.22), channel_id=1, replica_groups=mesh['leaf'=8,'rows'=4] {'leaf'}, dimensions={0} | all-to-all | bytes 32768 | tf_op jit(solution)/shard_map/all_to_all | solution.py:214
  58.5 0.6 shard_map.99
  59.1 0.0 copy-done.4
  59.1 0.0 copy-done.1
  59.1 0.0 copy-start.7
  59.1 0.0 copy-start.5
  59.1 9.1 %all_to_all.41 = bf16[32,8,128]{2,1,0:T(8,128)(2,1)S(1)} all-to-all(bf16[32,8,128]{2,1,0:T(8,128)(2,1)S(1)} %bitcast.30), channel_id=1, replica_groups=mesh['leaf'=8,'rows'=4] {'leaf','rows'}, dimensions={0} | all-to-all | bytes 131072 | tf_op jit(solution)/shard_map/all_to_all | solution.py:203
  68.2 1.3 %shard_map.100 = (bf16[8,8,128]{2,1,0:T(8,128)(2,1)S(1)}, f32[8,128]{1,0:T(8,128)S(1)}) custom-call(s32[4]{0:T(128)} %and_select_fusion.sources_ref, bf16[8,4,8,128]{3,2,1,0:T(8,128)(2,1)S(1)} %bitcast.23, bf16[192,192]{1,0:T(8,128)(2,1)S(1)} %get-tuple-element.37.high_ref, bf16[192,192]{1,0:T(8,128)(2,1)S(1)} %get-tuple-element.36.low_ref, ...), custom_call_target="tpu_custom_call" | custom-call | tf_op jit(solution)/shard_map/pallas_call | solution.py:26
  69.5 0.0 copy-start.2
  69.6 9.1 %all_to_all.42.refs_2_ = bf16[8,8,128]{2,1,0:T(8,128)(2,1)S(1)} all-to-all(bf16[8,8,128]{2,1,0:T(8,128)(2,1)S(1)} %get-tuple-element.27), channel_id=1, replica_groups=mesh['leaf'=8,'rows'=4] {'leaf'}, dimensions={0} | all-to-all | bytes 32768 | tf_op jit(solution)/shard_map/all_to_all | solution.py:214
  78.6 0.0 copy-done.7
  78.6 0.0 copy-done.5
  78.6 0.6 shard_map.101
  79.2 0.0 copy-start.8
  79.3 9.1 %all_to_all.43 = bf16[32,8,128]{2,1,0:T(8,128)(2,1)S(1)} all-to-all(bf16[32,8,128]{2,1,0:T(8,128)(2,1)S(1)} %bitcast.29), channel_id=1, replica_groups=mesh['leaf'=8,'rows'=4] {'leaf','rows'}, dimensions={0} | all-to-all | bytes 131072 | tf_op jit(solution)/shard_map/all_to_all | solution.py:203
  88.4 0.0 copy-done.2
  88.4 1.7 %shard_map.102 = (bf16[8,8,128]{2,1,0:T(8,128)(2,1)S(1)}, f32[8,128]{1,0:T(8,128)S(1)}) custom-call(s32[4]{0:T(128)} %and_select_fusion.sources_ref, bf16[8,4,8,128]{3,2,1,0:T(8,128)(2,1)S(1)} %bitcast.22, bf16[192,192]{1,0:T(8,128)(2,1)S(1)} %get-tuple-element.37.high_ref, bf16[192,192]{1,0:T(8,128)(2,1)S(1)} %get-tuple-element.36.low_ref, ...), custom_call_target="tpu_custom_call" | custom-call | tf_op jit(solution)/shard_map/pallas_call | solution.py:26
  90.1 9.0 %all_to_all.44.refs_2_ = bf16[8,8,128]{2,1,0:T(8,128)(2,1)S(1)} all-to-all(bf16[8,8,128]{2,1,0:T(8,128)(2,1)S(1)} %get-tuple-element.31), channel_id=1, replica_groups=mesh['leaf'=8,'rows'=4] {'leaf'}, dimensions={0} | all-to-all | bytes 32768 | tf_op jit(solution)/shard_map/all_to_all | solution.py:214
  99.0 1.0 shard_map.103
  (6 shorter events, 0.0 us)
Async XLA Ops:
  0.6 6.3 %copy-start = (bf16[1024,384]{1,0:T(8,128)(2,1)S(1)}, bf16[1024,384]{1,0:T(8,128)(2,1)}, u32[]{:S(2)}) copy-start(bf16[1024,384]{1,0:T(8,128)(2,1)} %param.12) | copy-start | bytes 2359300
  1.8 21.4 %collective-permute-start = (bf16[384,192]{1,0:T(8,128)(2,1)S(1)}, bf16[384,192]{1,0:T(8,128)(2,1)S(1)}, u32[]{:S(2)}, u32[]{:S(2)}) collective-permute-start(bf16[384,192]{1,0:T(8,128)(2,1)S(1)} %copy.28.refs_0_), channel_id=1, source_target_pairs={{0,1},{1,2},{2,3},{3,0},{4,5},{5,6},{6,7},{7,4},{8,9},{9,10},{10,1... | collective-permute-start | bytes 442376 | tf_op jit(solution)/shard_map/ppermute | solution.py:173
  2.3 20.8 %collective-permute-start.1 = (bf16[384,192]{1,0:T(8,128)(2,1)S(1)}, bf16[384,192]{1,0:T(8,128)(2,1)S(1)}, u32[]{:S(2)}, u32[]{:S(2)}) collective-permute-start(bf16[384,192]{1,0:T(8,128)(2,1)S(1)} %copy.28.refs_0_), channel_id=1, source_target_pairs={{0,2},{1,3},{2,0},{3,1},{4,6},{5,7},{6,4},{7,5},{8,10},{9,11},{10,... | collective-permute-start | bytes 442376 | tf_op jit(solution)/shard_map/ppermute | solution.py:173
  4.9 18.3 %collective-permute-start.2 = (bf16[384,192]{1,0:T(8,128)(2,1)S(1)}, bf16[384,192]{1,0:T(8,128)(2,1)S(1)}, u32[]{:S(2)}, u32[]{:S(2)}) collective-permute-start(bf16[384,192]{1,0:T(8,128)(2,1)S(1)} %copy.28.refs_0_), channel_id=1, source_target_pairs={{0,3},{1,0},{2,1},{3,2},{4,7},{5,4},{6,5},{7,6},{8,11},{9,8},{10,9... | collective-permute-start | bytes 442376 | tf_op jit(solution)/shard_map/ppermute | solution.py:173
  7.0 1.1 %copy-start.11 = (s32[8]{0:T(128)S(1)}, s32[8]{0:T(128)}, u32[]{:S(2)}) copy-start(s32[8]{0:T(128)} %param.11) | copy-start | bytes 100
  9.2 0.8 copy-start.3
  9.2 0.8 copy-start.6
  9.6 6.2 %copy-start.9 = (bf16[48,1024]{1,0:T(8,128)(2,1)S(1)}, bf16[48,1024]{1,0:T(8,128)(2,1)}, u32[]{:S(2)}) copy-start(bf16[48,1024]{1,0:T(8,128)(2,1)} %param.15) | copy-start | bytes 294916
  10.8 12.3 %all-to-all-start = ((bf16[32,8,128]{2,1,0:T(8,128)(2,1)}), bf16[32,8,128]{2,1,0:T(8,128)(2,1)S(1)}, u32[]{:S(2)}, u32[]{:S(2)}) async-start(bf16[32,8,128]{2,1,0:T(8,128)(2,1)} %bitcast.5), calls=%async_computation | async-start | bytes 131072 | tf_op jit(solution)/shard_map/all_to_all | solution.py:203
  21.6 8.4 %copy-start.10 = (bf16[384,192]{0,1:T(8,128)(2,1)S(1)}, bf16[384,192]{0,1:T(8,128)(2,1)}, u32[]{:S(2)}) copy-start(bf16[384,192]{0,1:T(8,128)(2,1)} %param.13) | copy-start | bytes 442372
  25.1 11.5 %all-to-all-start.1 = ((bf16[8,8,128]{2,1,0:T(8,128)(2,1)}), bf16[8,8,128]{2,1,0:T(8,128)(2,1)S(1)}, u32[]{:S(2)}, u32[]{:S(2)}) async-start(bf16[8,8,128]{2,1,0:T(8,128)(2,1)} %get-tuple-element.19), calls=%async_computation.1 | async-start | bytes 32768 | tf_op jit(solution)/shard_map/all_to_all | solution.py:214
  30.2 10.2 %collective-permute-start.3 = (bf16[384,192]{1,0:T(8,128)(2,1)S(1)}, bf16[384,192]{1,0:T(8,128)(2,1)S(1)}, u32[]{:S(2)}, u32[]{:S(2)}) collective-permute-start(bf16[384,192]{1,0:T(8,128)(2,1)S(1)} %copy.33.refs_0_), channel_id=1, source_target_pairs={{0,1},{1,2},{2,3},{3,0},{4,5},{5,6},{6,7},{7,4},{8,9},{9,10},{10,1... | collective-permute-start | bytes 442376 | tf_op jit(solution)/shard_map/ppermute | solution.py:173
  30.3 10.1 %collective-permute-start.4 = (bf16[384,192]{1,0:T(8,128)(2,1)S(1)}, bf16[384,192]{1,0:T(8,128)(2,1)}, u32[]{:S(2)}, u32[]{:S(2)}) collective-permute-start(bf16[384,192]{1,0:T(8,128)(2,1)S(1)} %copy.33.refs_0_), channel_id=1, source_target_pairs={{0,2},{1,3},{2,0},{3,1},{4,6},{5,7},{6,4},{7,5},{8,10},{9,11},{10,... | collective-permute-start | bytes 442376 | tf_op jit(solution)/shard_map/ppermute | solution.py:173
  31.8 8.9 %collective-permute-start.5 = (bf16[384,192]{1,0:T(8,128)(2,1)S(1)}, bf16[384,192]{1,0:T(8,128)(2,1)}, u32[]{:S(2)}, u32[]{:S(2)}) collective-permute-start(bf16[384,192]{1,0:T(8,128)(2,1)S(1)} %copy.33.refs_0_), channel_id=1, source_target_pairs={{0,3},{1,0},{2,1},{3,2},{4,7},{5,4},{6,5},{7,6},{8,11},{9,8},{10,9... | collective-permute-start | bytes 442376 | tf_op jit(solution)/shard_map/ppermute | solution.py:173
  37.8 21.2 %copy-start.4 = (f32[8,1024]{1,0:T(8,128)}, f32[8,1024]{1,0:T(8,128)S(1)}, u32[]{:S(2)}) copy-start(f32[8,1024]{1,0:T(8,128)S(1)} %get-tuple-element.25.refs_5_.refs_4_) | copy-start | bytes 98308
  37.8 10.0 %all-to-all-start.2 = ((bf16[32,8,128]{2,1,0:T(8,128)(2,1)}), bf16[32,8,128]{2,1,0:T(8,128)(2,1)S(1)}, u32[]{:S(2)}, u32[]{:S(2)}) async-start(bf16[32,8,128]{2,1,0:T(8,128)(2,1)} %bitcast.8), calls=%async_computation.2 | async-start | bytes 131072 | tf_op jit(solution)/shard_map/all_to_all | solution.py:203
  40.4 18.7 %copy-start.1 = (bf16[384,192]{1,0:T(8,128)(2,1)}, bf16[384,192]{1,0:T(8,128)(2,1)S(1)}, u32[]{:S(2)}) copy-start(bf16[384,192]{1,0:T(8,128)(2,1)S(1)} %collective-permute-done.3.refs_1_) | copy-start | bytes 442372
  59.1 19.6 %copy-start.7 = (f32[8,1024]{1,0:T(8,128)}, f32[8,1024]{1,0:T(8,128)S(1)}, u32[]{:S(2)}) copy-start(f32[8,1024]{1,0:T(8,128)S(1)} %get-tuple-element.35.refs_7_) | copy-start | bytes 98308
  59.1 19.6 %copy-start.5 = (f32[8,1024]{1,0:T(8,128)S(1)}, f32[8,1024]{1,0:T(8,128)}, u32[]{:S(2)}) copy-start(f32[8,1024]{1,0:T(8,128)} %copy-done.4) | copy-start | bytes 98308
  69.5 18.8 %copy-start.2 = (bf16[384,192]{1,0:T(8,128)(2,1)S(1)}, bf16[384,192]{1,0:T(8,128)(2,1)}, u32[]{:S(2)}) copy-start(bf16[384,192]{1,0:T(8,128)(2,1)} %copy-done.1) | copy-start | bytes 442372
  79.2 19.8 %copy-start.8 = (f32[8,1024]{1,0:T(8,128)S(1)}, f32[8,1024]{1,0:T(8,128)}, u32[]{:S(2)}) copy-start(f32[8,1024]{1,0:T(8,128)} %copy-done.7) | copy-start | bytes 98308

commit v4 on v3

--- a/solution.py
+++ b/solution.py
@@ -54,6 +54,22 @@
     lane = lax.broadcasted_iota(jnp.int32, carried.shape, 1)
     carried = jnp.where((lane >= rank_size) & (lane < rank_size + 3), carried, 0.0)
     return joined, jnp.sum(carried, axis=1, keepdims=True)
+
+
+def place_columns(local_index, slots, col_factor):
+    def body(index_ref, slots_ref, factor_ref, out_ref):
+        points, wide = out_ref.shape
+        ids = lax.broadcasted_iota(jnp.int32, (points, points), 0)
+        place = (ids == index_ref[...]).astype(F32).astype(BF16)
+        placed = jnp.dot(place, factor_ref[...], preferred_element_type=F32).astype(BF16)
+        ids = lax.broadcasted_iota(jnp.int32, (wide, wide), 0)
+        move = (ids == slots_ref[...]).astype(F32).astype(BF16)
+        out_ref[...] = jnp.dot(placed, move, preferred_element_type=F32).astype(BF16)
+
+    near = col_factor.size * col_factor.dtype.itemsize <= NEAR_BYTES
+    kind = pltpu.VMEM if near else jax.ShapeDtypeStruct
+    args = (local_index[None, :], slots[None, :], col_factor)
+    return call(body, args, kind(col_factor.shape, BF16))
 
 
 def middle_stage(sources, incoming, gram_high, gram_low, pieces, rank_size):
@@ -173,30 +189,9 @@
             pieces.append(lax.ppermute(block, "rows", ring))
         return pieces
 
-    own_gram = jnp.dot(row_factor, row_factor.T, preferred_element_type=F32)
-    grams = lax.all_gather(own_gram[None], "rows", axis=0, tiled=True)
-    pre_pieces = gather_rows(pre_factor)
-    mid_pieces = gather_rows(mid_factor)
-    same = (shifts[:, None] == shifts[None, :]).astype(F32)
-    gram = grams[:, :, None, :] * same[:, None, :, None]
-    gram = gram.reshape(row_count * rank_size, row_count * rank_size)
-    gram_high = lax.reduce_precision(gram, 8, 7)
-    gram_low = (gram - gram_high).astype(BF16)
-    gram_high = gram_high.astype(BF16)
-
     local_index = tree_order % points
-    point_ids = jnp.arange(points, dtype=jnp.int32)
-    place = (point_ids[:, None] == local_index[None, :]).astype(BF16)
-    columns = jnp.dot(place, col_factor, preferred_element_type=F32).astype(BF16)
-    slot_ids = jnp.arange(leaves, dtype=jnp.int32)
-    onehot = (mid_perm[:, None] == slot_ids[None, :]).astype(BF16)
-    columns = jnp.einsum(
-        "qg,ngk->nqk",
-        onehot,
-        columns.reshape(points, leaves, rank_size),
-        preferred_element_type=F32,
-    ).astype(BF16)
-    columns = columns.reshape(points, leaves * rank_size)
+    slots = (mid_perm[:, None] * rank_size + jnp.arange(rank_size)[None, :]).reshape(-1)
+    columns = place_columns(local_index, slots, col_factor)
     sizes = (leaves, row_count, sides, points, rank_size, width)
 
     def exchange(outgoing, pieces):
@@ -218,7 +213,20 @@
         return block_stage(update, state, columns, diagonal, *received, sizes, send, keep)
 
     (outgoing,) = stage(start_step, [right_side], (None, None), True, ())
+    row_factor, pre_factor, outgoing = lax.optimization_barrier(
+        (row_factor, pre_factor, outgoing)
+    )
+    own_gram = jnp.dot(row_factor, row_factor.T, preferred_element_type=F32)
+    pre_pieces = gather_rows(pre_factor)
+    grams = jnp.take(jnp.stack(gather_rows(own_gram)), sources, axis=0)
+    same = (shifts[:, None] == shifts[None, :]).astype(F32)
+    gram = grams[:, :, None, :] * same[:, None, :, None]
+    gram = gram.reshape(row_count * rank_size, row_count * rank_size)
+    gram_high = lax.reduce_precision(gram, 8, 7)
+    gram_low = (gram - gram_high).astype(BF16)
+    gram_high = gram_high.astype(BF16)
     received = exchange(outgoing, pre_pieces)
+    mid_pieces = gather_rows(mid_factor)
     direction, residual_dot, outgoing = stage(
         first_direction, [right_side], received, True, (True, False)
     )

time: 101 us -> 99.7 us (0.987)
  blocking collectives: 50.6 us -> 45.1 us
  waiting for transfers between devices: 11.7 us -> 16 us
  matrix products: 1.84 us -> 0.13 us
  Pallas kernels: 11 us -> 12.1 us
    all_gather x1 -> x0, blocking collectives: 5.36 us -> none  [per_device(): grams = lax.all_gather(own_gram[None], 'rows', axis=0, tiled=True)]
    all_to_all x2, waiting for transfers between devices: 8.03 us -> 11.7 us  [exchange(): lax.all_to_all(outgoing.reshape(leaves * row_count, sides, width), ('leaf...]
    dot_general x2 -> x0, matrix products: 1.71 us -> none  [the longest x1 1.11 us: per_device(): jnp.dot(place, col_factor, preferred_element_type=F32).astype(BF16)]
    all_to_all x1, starting transfers between devices: 4.89 us -> 3.38 us  [exchange(): lax.all_to_all(returned, 'leaf', split_axis=0, concat_axis=0, tiled=True)]
    all_to_all x2, starting transfers between devices: 7.45 us -> 8.59 us  [exchange(): lax.all_to_all(outgoing.reshape(leaves * row_count, sides, width), ('leaf...]
    pallas_call x9 -> x10, Pallas kernels: 11 us -> 12.1 us  [call(): pl.pallas_call(body, in_specs=specs, out_specs=jax.tree.map(lambda _: VME...]
    ppermute x6 -> x9, starting transfers between devices: 7.53 us -> 8.52 us  [gather_rows(): pieces.append(lax.ppermute(block, 'rows', ring))]
  transfers between devices with their start and end apart: 9 -> 12, of which waited for: 4 -> 3; matrix products, arithmetic and copies ran while one was open for 4% -> 2% of each run, Pallas kernels for 2% -> 1%
where the time goes in v4:
time: 99.7 us; the launch traced here: 99.1 us
  blocking collectives  45.1 us (45%)
  starting transfers between devices  20.5 us (21%)
  waiting for transfers between devices  16 us (16%)
  Pallas kernels  12.1 us (12%)
  local copies, waits for them, and re-layouts  2.82 us (3%)
  other arithmetic  1.58 us (2%)
    all_to_all x3, blocking collectives, exchange(): lax.all_to_all(returned, 'leaf', split_axis=0, concat_axis=0, tiled=True)  26.9 us
    all_to_all x2, blocking collectives, exchange(): lax.all_to_all(outgoing.reshape(leaves * row_count, sides, width), ('leaf...  18.2 us
    pallas_call x10, Pallas kernels, call(): pl.pallas_call(body, in_specs=specs, out_specs=jax.tree.map(lambda _: VME...  12.1 us
    all_to_all x2, waiting for transfers between devices, exchange(): lax.all_to_all(outgoing.reshape(leaves * row_count, sides, width), ('leaf...  11.7 us
    all_to_all x2, starting transfers between devices, exchange(): lax.all_to_all(outgoing.reshape(leaves * row_count, sides, width), ('leaf...  8.59 us
    ppermute x9, starting transfers between devices, gather_rows(): pieces.append(lax.ppermute(block, 'rows', ring))  8.52 us
    all_to_all x1, waiting for transfers between devices, exchange(): lax.all_to_all(returned, 'leaf', split_axis=0, concat_axis=0, tiled=True)  4.34 us
    all_to_all x1, starting transfers between devices, exchange(): lax.all_to_all(returned, 'leaf', split_axis=0, concat_axis=0, tiled=True)  3.38 us
  transfers between devices with their start and end apart: 12, of which 3 were waited for; matrix products, arithmetic and copies ran while one was open for 2% of the time, Pallas kernels for 1%

profile of v4, /device:TPU:0, one launch (start us, length us, event | category | flops | bytes accessed | tf_op | source)
XLA Modules:
  0.0 99.1 jit_solution(3703419454402122976)
XLA Ops:
  0.6 0.0 copy-start
  0.6 0.7 broadcast_multiply_fusion.1
  1.3 0.0 copy-start.6
  1.3 0.1 iota_add_fusion
  1.4 0.1 add.65.slots_ref
  1.5 0.5 copy-done.6
  2.0 0.0 copy-start.1
  2.0 1.1 %copy-done.1 = bf16[1024,384]{1,0:T(8,128)(2,1)S(1)} copy-done((bf16[1024,384]{1,0:T(8,128)(2,1)S(1)}, bf16[1024,384]{1,0:T(8,128)(2,1)}, u32[]{:S(2)}) %copy-start.1) | copy-done | bytes 786456
  3.2 0.0 copy-start.2
  3.2 0.0 copy-start.3
  3.2 1.7 %shard_map.95.refs_0_ = bf16[1024,384]{1,0:T(8,128)(2,1)S(1)} custom-call(s32[1,1024]{1,0:T(1,128)S(1)} %bitcast.29, s32[1,384]{1,0:T(1,128)S(1)} %add.65.slots_ref, bf16[1024,384]{1,0:T(8,128)(2,1)S(1)} %copy-done.1), custom_call_target="tpu_custom_call" | custom-call | tf_op jit(solution)/shard_map/pallas_call | solution.py:26
  4.9 0.0 copy-done.2
  4.9 0.0 copy-done.3
  4.9 0.9 shard_map.96
  5.9 0.0 copy-done
  5.9 0.0 copy-start.4
  5.9 0.1 fusion.6
  6.0 0.5 collective-permute-start
  6.6 2.6 %collective-permute-start.1 = (f32[48,48]{1,0:T(8,128)S(1)}, f32[48,48]{1,0:T(8,128)S(1)}, u32[]{:S(2)}, u32[]{:S(2)}) collective-permute-start(f32[48,48]{1,0:T(8,128)S(1)} %fusion.6), channel_id=1, source_target_pairs={{0,2},{1,3},{2,0},{3,1},{4,6},{5,7},{6,4},{7,5},{8,10},{9,11},{10,... | collective-permute-start | bytes 27656 | tf_op jit(solution)/shard_map/ppermute | solution.py:189
  9.1 1.4 %collective-permute-start.2 = (f32[48,48]{1,0:T(8,128)S(1)}, f32[48,48]{1,0:T(8,128)S(1)}, u32[]{:S(2)}, u32[]{:S(2)}) collective-permute-start(f32[48,48]{1,0:T(8,128)S(1)} %fusion.6), channel_id=1, source_target_pairs={{0,3},{1,0},{2,1},{3,2},{4,7},{5,4},{6,5},{7,6},{8,11},{9,8},{10,9... | collective-permute-start | bytes 27656 | tf_op jit(solution)/shard_map/ppermute | solution.py:189
  10.5 0.0 copy-done.4
  10.5 0.1 copy.13.refs_0_
  10.7 0.1 collective-permute-start.3
  10.7 0.4 collective-permute-start.4
  11.1 6.0 %all-to-all-start = ((bf16[32,8,128]{2,1,0:T(8,128)(2,1)}), bf16[32,8,128]{2,1,0:T(8,128)(2,1)S(1)}, u32[]{:S(2)}, u32[]{:S(2)}) async-start(bf16[32,8,128]{2,1,0:T(8,128)(2,1)} %bitcast.2), calls=%async_computation | async-start | bytes 131072 | tf_op jit(solution)/shard_map/all_to_all | solution.py:198
  17.2 0.5 and_select_fusion.1.sources_ref
  17.8 0.0 collective-permute-done
  17.8 1.5 %collective-permute-start.5 = (bf16[384,192]{1,0:T(8,128)(2,1)S(1)}, bf16[384,192]{1,0:T(8,128)(2,1)S(1)}, u32[]{:S(2)}, u32[]{:S(2)}) collective-permute-start(bf16[384,192]{1,0:T(8,128)(2,1)S(1)} %copy.13.refs_0_), channel_id=1, source_target_pairs={{0,3},{1,0},{2,1},{3,2},{4,7},{5,4},{6,5},{7,6},{8,11},{9,8},{10,9... | collective-permute-start | bytes 442376 | tf_op jit(solution)/shard_map/ppermute | solution.py:189
  19.3 0.0 collective-permute-done.1
  19.3 0.0 collective-permute-done.2
  19.3 0.6 gather_fusion
  19.8 0.1 broadcast_select_fusion
  19.9 0.1 broadcast_multiply_fusion
  20.1 0.2 mul.25
  20.3 4.3 %all-to-all-done = bf16[32,8,128]{2,1,0:T(8,128)(2,1)S(1)} async-done(((bf16[32,8,128]{2,1,0:T(8,128)(2,1)}), bf16[32,8,128]{2,1,0:T(8,128)(2,1)S(1)}, u32[]{:S(2)}, u32[]{:S(2)}) %all-to-all-start) | async-done | bytes 65568 | tf_op jit(solution)/shard_map/all_to_all | solution.py:198
  24.6 0.0 collective-permute-done.3.refs_1_
  24.6 0.0 collective-permute-done.4.refs_2_
  24.6 0.0 collective-permute-done.5.refs_3_
  24.6 0.0 copy-start.5
  24.6 2.1 %shard_map.97 = (bf16[8,8,128]{2,1,0:T(8,128)(2,1)}, f32[8,128]{1,0:T(8,128)S(1)}) custom-call(s32[4]{0:T(128)} %and_select_fusion.1.sources_ref, bf16[8,4,8,128]{3,2,1,0:T(8,128)(2,1)S(1)} %bitcast.18, bf16[192,192]{1,0:T(8,128)(2,1)S(1)} %get-tuple-element.43.high_ref, bf16[192,192]{1,0:T(8,128)(2,1)S(1)} %get-tuple-element.42.low_ref, ...), custom_call_target="tpu_custom_call" | custom-call | tf_op jit(solution)/shard_map/pallas_call | solution.py:26
  26.7 3.4 %all-to-all-start.1 = ((bf16[8,8,128]{2,1,0:T(8,128)(2,1)}), bf16[8,8,128]{2,1,0:T(8,128)(2,1)S(1)}, u32[]{:S(2)}, u32[]{:S(2)}) async-start(bf16[8,8,128]{2,1,0:T(8,128)(2,1)} %get-tuple-element.25), calls=%async_computation.1 | async-start | bytes 32768 | tf_op jit(solution)/shard_map/all_to_all | solution.py:209
  30.1 0.0 copy-done.5
  30.1 0.1 copy.17.refs_0_
  30.3 0.6 collective-permute-start.6
  30.8 1.5 %collective-permute-start.7 = (bf16[384,192]{1,0:T(8,128)(2,1)S(1)}, bf16[384,192]{1,0:T(8,128)(2,1)S(1)}, u32[]{:S(2)}, u32[]{:S(2)}) collective-permute-start(bf16[384,192]{1,0:T(8,128)(2,1)S(1)} %copy.17.refs_0_), channel_id=1, source_target_pairs={{0,2},{1,3},{2,0},{3,1},{4,6},{5,7},{6,4},{7,5},{8,10},{9,11},{10,... | collective-permute-start | bytes 442376 | tf_op jit(solution)/shard_map/ppermute | solution.py:189
  32.3 0.0 collective-permute-start.8
  32.3 4.3 %all-to-all-done.1.refs_2_ = bf16[8,8,128]{2,1,0:T(8,128)(2,1)S(1)} async-done(((bf16[8,8,128]{2,1,0:T(8,128)(2,1)}), bf16[8,8,128]{2,1,0:T(8,128)(2,1)S(1)}, u32[]{:S(2)}, u32[]{:S(2)}) %all-to-all-start.1) | async-done | bytes 16416 | tf_op jit(solution)/shard_map/all_to_all | solution.py:209
  36.7 1.2 %shard_map.98 = (f32[8,1024]{1,0:T(8,128)S(1)}, f32[8,128]{1,0:T(8,128)S(1)}, bf16[8,4,8,128]{3,2,1,0:T(8,128)(2,1)}) custom-call(bf16[1024,384]{1,0:T(8,128)(2,1)S(1)} %shard_map.95.refs_0_, f32[1,1024]{1,0:T(1,128)S(1)} %bitcast.23, bf16[8,8,128]{2,1,0:T(8,128)(2,1)S(1)} %all-to-all-done.1.refs_2_, f32[8,128]{1,0:T(8,128)S(1)} %get-tuple-element.26.refs_3_, ...), custom_call_target="tpu_custom_call" | custom-call | tf_op jit(solution)/shard_map/pallas_call | solution.py:26
  37.9 2.6 %all-to-all-start.2 = ((bf16[32,8,128]{2,1,0:T(8,128)(2,1)}), bf16[32,8,128]{2,1,0:T(8,128)(2,1)S(1)}, u32[]{:S(2)}, u32[]{:S(2)}) async-start(bf16[32,8,128]{2,1,0:T(8,128)(2,1)} %bitcast.9), calls=%async_computation.2 | async-start | bytes 131072 | tf_op jit(solution)/shard_map/all_to_all | solution.py:198
  40.4 0.0 collective-permute-done.6.refs_1_
  40.5 0.0 collective-permute-done.7.refs_2_
  40.5 0.0 collective-permute-done.8.refs_3_
  40.5 7.4 %all-to-all-done.2 = bf16[32,8,128]{2,1,0:T(8,128)(2,1)S(1)} async-done(((bf16[32,8,128]{2,1,0:T(8,128)(2,1)}), bf16[32,8,128]{2,1,0:T(8,128)(2,1)S(1)}, u32[]{:S(2)}, u32[]{:S(2)}) %all-to-all-start.2) | async-done | bytes 65568 | tf_op jit(solution)/shard_map/all_to_all | solution.py:198
  47.9 1.3 %shard_map.99 = (bf16[8,8,128]{2,1,0:T(8,128)(2,1)S(1)}, f32[8,128]{1,0:T(8,128)S(1)}) custom-call(s32[4]{0:T(128)} %and_select_fusion.1.sources_ref, bf16[8,4,8,128]{3,2,1,0:T(8,128)(2,1)S(1)} %bitcast.19, bf16[192,192]{1,0:T(8,128)(2,1)S(1)} %get-tuple-element.43.high_ref, bf16[192,192]{1,0:T(8,128)(2,1)S(1)} %get-tuple-element.42.low_ref, ...), custom_call_target="tpu_custom_call" | custom-call | tf_op jit(solution)/shard_map/pallas_call | solution.py:26
  49.2 9.0 %all_to_all.40.refs_2_ = bf16[8,8,128]{2,1,0:T(8,128)(2,1)S(1)} all-to-all(bf16[8,8,128]{2,1,0:T(8,128)(2,1)S(1)} %get-tuple-element.28), channel_id=1, replica_groups=mesh['leaf'=8,'rows'=4] {'leaf'}, dimensions={0} | all-to-all | bytes 32768 | tf_op jit(solution)/shard_map/all_to_all | solution.py:209
  58.2 0.6 shard_map.100
  58.7 9.1 %all_to_all.41 = bf16[32,8,128]{2,1,0:T(8,128)(2,1)S(1)} all-to-all(bf16[32,8,128]{2,1,0:T(8,128)(2,1)S(1)} %bitcast.28), channel_id=1, replica_groups=mesh['leaf'=8,'rows'=4] {'leaf','rows'}, dimensions={0} | all-to-all | bytes 131072 | tf_op jit(solution)/shard_map/all_to_all | solution.py:198
  67.9 1.3 %shard_map.101 = (bf16[8,8,128]{2,1,0:T(8,128)(2,1)S(1)}, f32[8,128]{1,0:T(8,128)S(1)}) custom-call(s32[4]{0:T(128)} %and_select_fusion.1.sources_ref, bf16[8,4,8,128]{3,2,1,0:T(8,128)(2,1)S(1)} %bitcast.21, bf16[192,192]{1,0:T(8,128)(2,1)S(1)} %get-tuple-element.43.high_ref, bf16[192,192]{1,0:T(8,128)(2,1)S(1)} %get-tuple-element.42.low_ref, ...), custom_call_target="tpu_custom_call" | custom-call | tf_op jit(solution)/shard_map/pallas_call | solution.py:26
  69.2 9.0 %all_to_all.42.refs_2_ = bf16[8,8,128]{2,1,0:T(8,128)(2,1)S(1)} all-to-all(bf16[8,8,128]{2,1,0:T(8,128)(2,1)S(1)} %get-tuple-element.33), channel_id=1, replica_groups=mesh['leaf'=8,'rows'=4] {'leaf'}, dimensions={0} | all-to-all | bytes 32768 | tf_op jit(solution)/shard_map/all_to_all | solution.py:209
  78.2 0.6 shard_map.102
  78.8 9.1 %all_to_all.43 = bf16[32,8,128]{2,1,0:T(8,128)(2,1)S(1)} all-to-all(bf16[32,8,128]{2,1,0:T(8,128)(2,1)S(1)} %bitcast.27), channel_id=1, replica_groups=mesh['leaf'=8,'rows'=4] {'leaf','rows'}, dimensions={0} | all-to-all | bytes 131072 | tf_op jit(solution)/shard_map/all_to_all | solution.py:198
  87.9 1.3 %shard_map.103 = (bf16[8,8,128]{2,1,0:T(8,128)(2,1)S(1)}, f32[8,128]{1,0:T(8,128)S(1)}) custom-call(s32[4]{0:T(128)} %and_select_fusion.1.sources_ref, bf16[8,4,8,128]{3,2,1,0:T(8,128)(2,1)S(1)} %bitcast.20, bf16[192,192]{1,0:T(8,128)(2,1)S(1)} %get-tuple-element.43.high_ref, bf16[192,192]{1,0:T(8,128)(2,1)S(1)} %get-tuple-element.42.low_ref, ...), custom_call_target="tpu_custom_call" | custom-call | tf_op jit(solution)/shard_map/pallas_call | solution.py:26
  89.2 9.0 %all_to_all.44.refs_2_ = bf16[8,8,128]{2,1,0:T(8,128)(2,1)S(1)} all-to-all(bf16[8,8,128]{2,1,0:T(8,128)(2,1)S(1)} %get-tuple-element.37), channel_id=1, replica_groups=mesh['leaf'=8,'rows'=4] {'leaf'}, dimensions={0} | all-to-all | bytes 32768 | tf_op jit(solution)/shard_map/all_to_all | solution.py:209
  98.2 1.0 shard_map.104
  (7 shorter events, 0.1 us)
Async XLA Ops:
  0.6 5.2 %copy-start = (bf16[48,1024]{1,0:T(8,128)(2,1)S(1)}, bf16[48,1024]{1,0:T(8,128)(2,1)}, u32[]{:S(2)}) copy-start(bf16[48,1024]{1,0:T(8,128)(2,1)} %param.15) | copy-start | bytes 294916
  1.3 0.7 copy-start.6
  2.0 1.1 %copy-start.1 = (bf16[1024,384]{1,0:T(8,128)(2,1)S(1)}, bf16[1024,384]{1,0:T(8,128)(2,1)}, u32[]{:S(2)}) copy-start(bf16[1024,384]{1,0:T(8,128)(2,1)} %factor_ref.1) | copy-start | bytes 2359300
  3.2 1.8 %copy-start.2 = (f32[8,1024]{1,0:T(8,128)S(1)}, f32[8,1024]{1,0:T(8,128)}, u32[]{:S(2)}) copy-start(f32[8,1024]{1,0:T(8,128)} %refs_6_.1) | copy-start | bytes 98308
  3.2 1.8 %copy-start.3 = (f32[1024]{0:T(1024)S(1)}, f32[1024]{0:T(1024)}, u32[]{:S(2)}) copy-start(f32[1024]{0:T(1024)} %param.9) | copy-start | bytes 12292
  5.9 4.7 %copy-start.4 = (bf16[384,192]{0,1:T(8,128)(2,1)S(1)}, bf16[384,192]{0,1:T(8,128)(2,1)}, u32[]{:S(2)}) copy-start(bf16[384,192]{0,1:T(8,128)(2,1)} %param.14) | copy-start | bytes 442372
  6.0 11.8 %collective-permute-start = (f32[48,48]{1,0:T(8,128)S(1)}, f32[48,48]{1,0:T(8,128)S(1)}, u32[]{:S(2)}, u32[]{:S(2)}) collective-permute-start(f32[48,48]{1,0:T(8,128)S(1)} %fusion.6), channel_id=1, source_target_pairs={{0,1},{1,2},{2,3},{3,0},{4,5},{5,6},{6,7},{7,4},{8,9},{9,10},{10,1... | collective-permute-start | bytes 27656 | tf_op jit(solution)/shard_map/ppermute | solution.py:189
  6.6 12.7 %collective-permute-start.1 = (f32[48,48]{1,0:T(8,128)S(1)}, f32[48,48]{1,0:T(8,128)S(1)}, u32[]{:S(2)}, u32[]{:S(2)}) collective-permute-start(f32[48,48]{1,0:T(8,128)S(1)} %fusion.6), channel_id=1, source_target_pairs={{0,2},{1,3},{2,0},{3,1},{4,6},{5,7},{6,4},{7,5},{8,10},{9,11},{10,... | collective-permute-start | bytes 27656 | tf_op jit(solution)/shard_map/ppermute | solution.py:189
  9.1 10.1 %collective-permute-start.2 = (f32[48,48]{1,0:T(8,128)S(1)}, f32[48,48]{1,0:T(8,128)S(1)}, u32[]{:S(2)}, u32[]{:S(2)}) collective-permute-start(f32[48,48]{1,0:T(8,128)S(1)} %fusion.6), channel_id=1, source_target_pairs={{0,3},{1,0},{2,1},{3,2},{4,7},{5,4},{6,5},{7,6},{8,11},{9,8},{10,9... | collective-permute-start | bytes 27656 | tf_op jit(solution)/shard_map/ppermute | solution.py:189
  10.7 13.9 %collective-permute-start.3 = (bf16[384,192]{1,0:T(8,128)(2,1)S(1)}, bf16[384,192]{1,0:T(8,128)(2,1)S(1)}, u32[]{:S(2)}, u32[]{:S(2)}) collective-permute-start(bf16[384,192]{1,0:T(8,128)(2,1)S(1)} %copy.13.refs_0_), channel_id=1, source_target_pairs={{0,1},{1,2},{2,3},{3,0},{4,5},{5,6},{6,7},{7,4},{8,9},{9,10},{10,1... | collective-permute-start | bytes 442376 | tf_op jit(solution)/shard_map/ppermute | solution.py:189
  10.7 13.8 %collective-permute-start.4 = (bf16[384,192]{1,0:T(8,128)(2,1)S(1)}, bf16[384,192]{1,0:T(8,128)(2,1)S(1)}, u32[]{:S(2)}, u32[]{:S(2)}) collective-permute-start(bf16[384,192]{1,0:T(8,128)(2,1)S(1)} %copy.13.refs_0_), channel_id=1, source_target_pairs={{0,2},{1,3},{2,0},{3,1},{4,6},{5,7},{6,4},{7,5},{8,10},{9,11},{10,... | collective-permute-start | bytes 442376 | tf_op jit(solution)/shard_map/ppermute | solution.py:189
  11.1 13.5 %all-to-all-start = ((bf16[32,8,128]{2,1,0:T(8,128)(2,1)}), bf16[32,8,128]{2,1,0:T(8,128)(2,1)S(1)}, u32[]{:S(2)}, u32[]{:S(2)}) async-start(bf16[32,8,128]{2,1,0:T(8,128)(2,1)} %bitcast.2), calls=%async_computation | async-start | bytes 131072 | tf_op jit(solution)/shard_map/all_to_all | solution.py:198
  17.8 6.8 %collective-permute-start.5 = (bf16[384,192]{1,0:T(8,128)(2,1)S(1)}, bf16[384,192]{1,0:T(8,128)(2,1)S(1)}, u32[]{:S(2)}, u32[]{:S(2)}) collective-permute-start(bf16[384,192]{1,0:T(8,128)(2,1)S(1)} %copy.13.refs_0_), channel_id=1, source_target_pairs={{0,3},{1,0},{2,1},{3,2},{4,7},{5,4},{6,5},{7,6},{8,11},{9,8},{10,9... | collective-permute-start | bytes 442376 | tf_op jit(solution)/shard_map/ppermute | solution.py:189
  24.6 5.5 %copy-start.5 = (bf16[384,192]{0,1:T(8,128)(2,1)S(1)}, bf16[384,192]{0,1:T(8,128)(2,1)}, u32[]{:S(2)}) copy-start(bf16[384,192]{0,1:T(8,128)(2,1)} %param.13) | copy-start | bytes 442372
  26.7 10.0 %all-to-all-start.1 = ((bf16[8,8,128]{2,1,0:T(8,128)(2,1)}), bf16[8,8,128]{2,1,0:T(8,128)(2,1)S(1)}, u32[]{:S(2)}, u32[]{:S(2)}) async-start(bf16[8,8,128]{2,1,0:T(8,128)(2,1)} %get-tuple-element.25), calls=%async_computation.1 | async-start | bytes 32768 | tf_op jit(solution)/shard_map/all_to_all | solution.py:209
  30.3 10.2 %collective-permute-start.6 = (bf16[384,192]{1,0:T(8,128)(2,1)S(1)}, bf16[384,192]{1,0:T(8,128)(2,1)S(1)}, u32[]{:S(2)}, u32[]{:S(2)}) collective-permute-start(bf16[384,192]{1,0:T(8,128)(2,1)S(1)} %copy.17.refs_0_), channel_id=1, source_target_pairs={{0,1},{1,2},{2,3},{3,0},{4,5},{5,6},{6,7},{7,4},{8,9},{9,10},{10,1... | collective-permute-start | bytes 442376 | tf_op jit(solution)/shard_map/ppermute | solution.py:189
  30.8 9.6 %collective-permute-start.7 = (bf16[384,192]{1,0:T(8,128)(2,1)S(1)}, bf16[384,192]{1,0:T(8,128)(2,1)S(1)}, u32[]{:S(2)}, u32[]{:S(2)}) collective-permute-start(bf16[384,192]{1,0:T(8,128)(2,1)S(1)} %copy.17.refs_0_), channel_id=1, source_target_pairs={{0,2},{1,3},{2,0},{3,1},{4,6},{5,7},{6,4},{7,5},{8,10},{9,11},{10,... | collective-permute-start | bytes 442376 | tf_op jit(solution)/shard_map/ppermute | solution.py:189
  32.3 8.1 %collective-permute-start.8 = (bf16[384,192]{1,0:T(8,128)(2,1)S(1)}, bf16[384,192]{1,0:T(8,128)(2,1)S(1)}, u32[]{:S(2)}, u32[]{:S(2)}) collective-permute-start(bf16[384,192]{1,0:T(8,128)(2,1)S(1)} %copy.17.refs_0_), channel_id=1, source_target_pairs={{0,3},{1,0},{2,1},{3,2},{4,7},{5,4},{6,5},{7,6},{8,11},{9,8},{10,9... | collective-permute-start | bytes 442376 | tf_op jit(solution)/shard_map/ppermute | solution.py:189
  37.9 10.0 %all-to-all-start.2 = ((bf16[32,8,128]{2,1,0:T(8,128)(2,1)}), bf16[32,8,128]{2,1,0:T(8,128)(2,1)S(1)}, u32[]{:S(2)}, u32[]{:S(2)}) async-start(bf16[32,8,128]{2,1,0:T(8,128)(2,1)} %bitcast.9), calls=%async_computation.2 | async-start | bytes 131072 | tf_op jit(solution)/shard_map/all_to_all | solution.py:198
